TPU v7x, 32 devices: a whole 2x2x4 slice. The times are simulated.
32 devices in a mesh: dp: 16 (over z, y, core), tensor: 2 (over x).
Axes of the slice: x: 2, y: 2, z: 4, core: 2. Of those that a mesh axis runs over, the one named last changes fastest.
Arguments:
- noisy_sample: float32 [2048, 28], P('dp'), may hold values from -5 to 5
- timestep: int32 [2048], P('dp'), may hold values from 0 to 99
- noise: float32 [2048, 28], P('dp'), may hold values from -5 to 5
- obs_feat: bfloat16 [2048, 1024], P('dp'), may hold values from -6 to 6
- step_w1: bfloat16 [256, 1024], replicated, may hold values from -0.75 to 0.75
- step_w2: bfloat16 [1024, 256], replicated, may hold values from -0.25 to 0.25
- film_weight: bfloat16 [1280, 2, 4096], P('dp', None, 'tensor'), may hold values from -0.25 to 0.25
- conv_in_w: bfloat16 [5, 7, 4096], P(None, None, 'tensor'), may hold values from -1 to 1
- residual_w: bfloat16 [7, 4096], P(None, 'tensor'), may hold values from -2 to 2
- conv_mid_w: bfloat16 [5, 4096, 4096], P(None, 'dp', 'tensor'), may hold values from -0.0390625 to 0.0390625
- out_w: bfloat16 [4096, 7], P('tensor'), may hold values from -0.1875 to 0.1875
- gain_one: float32 [4096], P('tensor'), may hold values from 0.4 to 1.6
- gain_two: float32 [4096], P('tensor'), may hold values from 0.4 to 1.6
Outputs:
- predicted_noise: float32 [2048, 28], P('dp')
- denoised: float32 [2048, 28], P('dp')
All inputs are finite; a program needn't handle non-finite values.
Results may differ from a plain program's by a relative error of at most 0.0046.
Values may be sent and summed in bfloat16 or wider, within the bound.
A program may use at most 192 MiB of HBM per device.

v0:
```python
import math

import jax
import jax.numpy as jnp
from jax import lax
from jax.experimental import pallas as pl
from jax.experimental.pallas import tpu as pltpu
from jax.sharding import Mesh
from jax.sharding import PartitionSpec as P

C = 4096
ACT = 7
HORIZON = 4
TAPS = 5
GROUPS = 8
STEP = 256
TRAIN_STEPS = 100


def plan():
    pos = jnp.arange(TRAIN_STEPS + 1, dtype=jnp.float32) / TRAIN_STEPS
    curve = jnp.cos((pos + 0.008) / 1.008 * (math.pi / 2)) ** 2
    betas = jnp.minimum(1.0 - curve[1:] / curve[:-1], 0.999)
    return jnp.cumprod(1.0 - betas)


def lookup(table, steps):
    onehot = (steps[:, None] == jnp.arange(table.shape[0], dtype=jnp.int32)[None, :]).astype(
        jnp.float32
    )
    return jnp.sum(onehot * table[None, :], axis=1)


def mish(value):
    e = jnp.exp(jnp.minimum(value, 20.0))
    n = e * (e + 2.0)
    return value * (n / (n + 2.0))


def sinusoid(steps):
    half = STEP // 2
    freqs = jnp.exp(jnp.arange(half, dtype=jnp.float32) * (-math.log(10000.0) / (half - 1)))
    angles = steps.astype(jnp.float32)[:, None] * freqs[None, :]
    return jnp.concatenate([jnp.sin(angles), jnp.cos(angles)], axis=1)


def denoise_step(sample, eps, noise, steps):
    alpha_bar = plan()
    now = lookup(alpha_bar, steps)[:, None]
    before = jnp.where(steps > 0, lookup(alpha_bar, jnp.maximum(steps - 1, 0)), 1.0)[:, None]
    beta_prod = 1.0 - now
    cur_alpha = now / before
    cur_beta = 1.0 - cur_alpha
    start = jnp.clip((sample - jnp.sqrt(beta_prod) * eps) / jnp.sqrt(now), -1.0, 1.0)
    mean = (
        jnp.sqrt(before) * cur_beta / beta_prod * start
        + jnp.sqrt(cur_alpha) * (1.0 - before) / beta_prod * sample
    )
    spread = jnp.sqrt((1.0 - before) / beta_prod * cur_beta)
    return mean + spread * noise


DEPTH_PARTS = 4
PARTS = 2
VMEM = 60 * 1024 * 1024


def first_kernel(blocks, x_ref, wt_ref, cond_ref, film_ref, gain_ref, out_ref):
    x = x_ref[...]
    hs = [
        jnp.dot(x, wt_ref[h], preferred_element_type=jnp.float32) for h in range(HORIZON)
    ]
    width = hs[0].shape[1]
    count = HORIZON * width
    mean = sum(jnp.sum(h, axis=1, keepdims=True) for h in hs) / count
    hs = [h - mean for h in hs]
    var = sum(jnp.sum(h * h, axis=1, keepdims=True) for h in hs) / count
    inv = 1.0 / jnp.sqrt(var + 1e-05)
    cond = cond_ref[...]
    scale = jnp.dot(cond, film_ref[0], preferred_element_type=jnp.float32)
    shift = jnp.dot(cond, film_ref[1], preferred_element_type=jnp.float32)
    gain = gain_ref[...]
    cl = width // blocks
    for h in range(HORIZON):
        val = (scale * mish(hs[h] * inv * gain) + shift).astype(jnp.bfloat16)
        for b in range(blocks):
            out_ref[b, :, h * cl : (h + 1) * cl] = val[:, b * cl : (b + 1) * cl]


def first_stage(xs, wt, cond, film, gain, blocks, cl):
    rows = xs.shape[0]
    width = wt.shape[2]
    gw = C // GROUPS
    per = gw // cl
    rt = min(128, rows)
    inner = cond.shape[1]
    kern = lambda *refs: first_kernel(per, *refs)
    return pl.pallas_call(
        kern,
        grid=(width // gw, rows // rt),
        in_specs=[
            pl.BlockSpec((rt, xs.shape[1]), lambda g, r: (r, 0)),
            pl.BlockSpec((HORIZON, wt.shape[1], gw), lambda g, r: (0, 0, g)),
            pl.BlockSpec((rt, inner), lambda g, r: (r, 0)),
            pl.BlockSpec((2, inner, gw), lambda g, r: (0, 0, g)),
            pl.BlockSpec((1, gw), lambda g, r: (0, g)),
        ],
        out_specs=pl.BlockSpec((per, rt, HORIZON * cl), lambda g, r: (g, r, 0)),
        out_shape=jax.ShapeDtypeStruct((blocks, rows, HORIZON * cl), jnp.bfloat16),
        compiler_params=pltpu.CompilerParams(vmem_limit_bytes=VMEM),
        cost_estimate=pl.CostEstimate(
            flops=4 * rows * inner * width,
            bytes_accessed=4 * inner * width + 2 * rows * width * HORIZON,
            transcendentals=rows * width * HORIZON,
        ),
        name="first_stage",
    )(xs, wt, cond, film, gain)


def mix_kernel(pieces, mid, order_ref, *refs):
    a_ref, w_refs, out_ref = refs[0], refs[1 : 1 + pieces], refs[1 + pieces]
    cl = w_refs[0].shape[0] // TAPS
    parts, _, rows, _ = out_ref.shape
    for h in range(HORIZON):
        p0 = max(0, h - mid)
        p1 = min(HORIZON, h - mid + TAPS)
        k0 = p0 - h + mid
        k1 = p1 - h + mid
        acc = None
        for i in range(pieces):
            left = a_ref[order_ref[i], :, p0 * cl : p1 * cl]
            term = jnp.dot(
                left, w_refs[i][k0 * cl : k1 * cl, :], preferred_element_type=jnp.float32
            )
            acc = term if acc is None else acc + term
        for q in range(parts):
            out_ref[q, h] = acc[q * rows : (q + 1) * rows].astype(jnp.bfloat16)


def mix(order, acts, pieces):
    n = len(pieces)
    rows = acts.shape[1]
    width = pieces[0].shape[1]
    nt = min(256, width)
    kern = lambda *refs: mix_kernel(n, TAPS // 2, *refs)
    return pl.pallas_call(
        kern,
        grid=(width // nt,),
        in_specs=[
            pl.BlockSpec(memory_space=pltpu.SMEM),
            pl.BlockSpec(acts.shape, lambda j: (0, 0, 0)),
        ]
        + [pl.BlockSpec((p.shape[0], nt), lambda j: (0, j)) for p in pieces],
        out_specs=pl.BlockSpec(
            (DEPTH_PARTS, HORIZON, rows // DEPTH_PARTS, nt), lambda j: (0, 0, 0, j)
        ),
        out_shape=jax.ShapeDtypeStruct(
            (DEPTH_PARTS, HORIZON, rows // DEPTH_PARTS, width), jnp.bfloat16
        ),
        compiler_params=pltpu.CompilerParams(vmem_limit_bytes=VMEM),
        cost_estimate=pl.CostEstimate(
            flops=2 * 14 * rows * n * pieces[0].shape[0] // TAPS * width,
            bytes_accessed=2 * n * pieces[0].shape[0] * width + 8 * rows * width,
            transcendentals=0,
        ),
        name="mix",
    )(order, acts, *pieces)


def hop(value, axis, step):
    size = lax.axis_size(axis)
    return lax.ppermute(value, axis, [(i, (i + step) % size) for i in range(size)])


def relative(value):
    return jnp.concatenate(
        [value] + [hop(value, "z", -q) for q in range(1, DEPTH_PARTS)], axis=0
    )


def reduce_parts(part):
    half = HORIZON // 2
    far = part[2]
    up = hop(far[:half], "z", 1)
    down = hop(far[half:], "z", -1)
    f32 = jnp.float32
    near_up = (part[1, :half].astype(f32) + up.astype(f32)).astype(jnp.bfloat16)
    near_down = (part[3, half:].astype(f32) + down.astype(f32)).astype(jnp.bfloat16)
    got = [
        (hop(near_up, "z", 1), hop(part[3, :half], "z", -1)),
        (hop(part[1, half:], "z", 1), hop(near_down, "z", -1)),
    ]
    out = []
    for h in range(HORIZON):
        one, two = got[h // half]
        out.append(
            part[0, h].astype(f32) + one[h % half].astype(f32) + two[h % half].astype(f32)
        )
    return out


def body(
    noisy_sample,
    timestep,
    noise,
    obs_feat,
    step_w1,
    step_w2,
    film_weight,
    conv_in_w,
    residual_w,
    conv_mid_w,
    out_w,
    gain_one,
    gain_two,
):
    count = noisy_sample.shape[0]
    local_width = conv_in_w.shape[2]
    cl = conv_mid_w.shape[1]
    yn = lax.axis_size("y")
    zi, yi, ci = lax.axis_index("z"), lax.axis_index("y"), lax.axis_index("c")
    blocks = yn * 2
    kw = cl * blocks
    step = local_width // PARTS
    pieces = []
    for n in range(PARTS):
        own = conv_mid_w.reshape(TAPS * cl, local_width)[:, n * step : (n + 1) * step]
        near = [own] + [hop(own, "y", -s) for s in range(1, yn)]
        pieces.append(near + [hop(v, "c", 1) for v in near])
    order = jnp.stack(
        [((yi + s) % yn) * 2 + ci for s in range(yn)]
        + [((yi + s) % yn) * 2 + (1 - ci) for s in range(yn)]
    ).astype(jnp.int32)
    film = jnp.transpose(film_weight, (1, 0, 2))
    film = lax.all_gather(film, "tensor", axis=2, tiled=True)
    film = lax.all_to_all(film, "z", split_axis=2, concat_axis=1, tiled=True)
    film = lax.all_gather(film, ("y", "c"), axis=1, tiled=True)
    win = lax.all_gather(conv_in_w, "tensor", axis=2, tiled=True)
    win = lax.dynamic_slice_in_dim(win, zi * kw, kw, 2)
    gain = lax.all_gather(gain_one, "tensor", axis=0, tiled=True)
    gain = lax.dynamic_slice_in_dim(gain, zi * kw, kw, 0)[None, :]
    toep = []
    for h in range(HORIZON):
        rows = []
        for p in range(HORIZON):
            k = p - h + TAPS // 2
            rows.append(win[k] if 0 <= k < TAPS else jnp.zeros((ACT, kw), win.dtype))
        toep.append(jnp.concatenate(rows, axis=0))
    toep = jnp.stack(toep)
    sample_b = noisy_sample.astype(jnp.bfloat16)
    sinus = sinusoid(timestep).astype(jnp.bfloat16)
    step_hidden = mish(jnp.dot(sinus, step_w1, preferred_element_type=jnp.float32)).astype(
        jnp.bfloat16
    )
    step_feat = jnp.dot(step_hidden, step_w2, preferred_element_type=jnp.float32)
    cond = mish(jnp.concatenate([step_feat, obs_feat.astype(jnp.float32)], axis=1)).astype(
        jnp.bfloat16
    )
    fr = film_weight.shape[0]
    cond = (
        cond.reshape(count, DEPTH_PARTS, blocks, fr)
        .transpose(0, 2, 1, 3)
        .reshape(count, cond.shape[1])
    )
    acts = first_stage(relative(sample_b), toep, relative(cond), film, gain, blocks, cl)
    found = [reduce_parts(mix(order, acts, p)) for p in pieces]
    hs = [jnp.concatenate([f[h] for f in found], axis=1) for h in range(HORIZON)]
    gw = C // GROUPS
    outs = []
    cols = [slice(g * gw, (g + 1) * gw) for g in range(local_width // gw)]
    stats = []
    for col in cols:
        mean = sum(jnp.sum(h[:, col], axis=1, keepdims=True) for h in hs) / (HORIZON * gw)
        var = sum(jnp.sum((h[:, col] - mean) ** 2, axis=1, keepdims=True) for h in hs) / (
            HORIZON * gw
        )
        stats.append((mean, 1.0 / jnp.sqrt(var + 1e-05)))
    mean = jnp.concatenate([jnp.broadcast_to(m, (count, gw)) for m, _ in stats], axis=1)
    inv = jnp.concatenate([jnp.broadcast_to(v, (count, gw)) for _, v in stats], axis=1)
    for h in range(HORIZON):
        skip = jnp.dot(
            sample_b[:, h * ACT : (h + 1) * ACT], residual_w, preferred_element_type=jnp.float32
        )
        normed = (hs[h] - mean) * inv * gain_two[None, :]
        act_two = (mish(normed) + skip).astype(jnp.bfloat16)
        outs.append(jnp.dot(act_two, out_w, preferred_element_type=jnp.float32))
    eps = lax.psum(jnp.concatenate(outs, axis=1), "tensor")
    denoised = denoise_step(noisy_sample, eps, noise, timestep)
    return (eps, denoised)


def solution(mesh):
    dp, tensor = mesh.shape["dp"], mesh.shape["tensor"]
    grid = Mesh(
        mesh.devices.reshape(DEPTH_PARTS, dp // DEPTH_PARTS // 2, 2, tensor),
        ("z", "y", "c", "tensor"),
    )
    rows = ("z", "y", "c")
    return jax.shard_map(
        body,
        mesh=grid,
        in_specs=(
            P(rows, None),
            P(rows),
            P(rows, None),
            P(rows, None),
            P(),
            P(),
            P(rows, None, "tensor"),
            P(None, None, "tensor"),
            P(None, "tensor"),
            P(None, rows, "tensor"),
            P("tensor", None),
            P("tensor"),
            P("tensor"),
        ),
        out_specs=(P(rows, None), P(rows, None)),
        check_vma=False,
    )
```

profile of v0, /device:TPU:0, one launch (start us, length us, event | category | flops | bytes accessed | tf_op | source)
XLA Modules:
  0.0 471.8 jit_solution(17640339304237799261)
XLA Ops:
  9.5 27.1 %all-gather.3.cloned.1.call-done = bf16[2,80,4096]{2,1,0:T(8,128)(2,1)} async-done(((bf16[2,80,2048]{2,1,0:T(8,128)(2,1)}), bf16[2,80,4096]{2,1,0:T(8,128)(2,1)}) %all-gather.3.cloned.1.call-update) | async-done | bytes 1310736 | tf_op jit(solution)/shard_map/all_gather | solution.py:235
  36.6 5.1 %copy.61 = bf16[2,80,4096]{1,0,2:T(2,128)(2,1)S(1)} copy(bf16[2,80,4096]{2,1,0:T(8,128)(2,1)} %all-gather.3.cloned.1.call-done) | data formatting | bytes 2621440 | tf_op jit(solution)/shard_map/all_gather | solution.py:235
  41.7 52.5 %all_to_all.18 = bf16[2,80,4096]{1,0,2:T(2,128)(2,1)} all-to-all(bf16[2,80,4096]{1,0,2:T(2,128)(2,1)S(1)} %copy.61), channel_id=1, replica_groups=mesh['z'=4,'y'=2,'c'=2,'tensor'=2] {'z'}, dimensions={2} | all-to-all | bytes 2621440 | tf_op jit(solution)/shard_map/all_to_all | solution.py:236
  94.2 6.0 %copy.62 = bf16[2,80,4,1024]{3,1,2,0:T(8,128)(2,1)} copy(bf16[2,80,4,1024]{1,0,3,2:T(2,128)(2,1)} %bitcast.203) | data formatting | bytes 2621440 | tf_op jit(solution)/shard_map/all_to_all | solution.py:236
  100.2 4.6 fusion.87
  108.8 84.1 %collective-permute-done.12.refs_3_ = bf16[1280,1024]{1,0:T(8,128)(2,1)} collective-permute-done((bf16[1280,1024]{1,0:T(8,128)(2,1)}, bf16[1280,1024]{1,0:T(8,128)(2,1)}, u32[]{:S(2)}, u32[]{:S(2)}) %collective-permute-start.12) | collective-permute-done | bytes 2621472 | tf_op jit(solution)/shard_map/ppermute | solution.py:172
  198.0 11.3 %collective-permute-done.2 = bf16[128,28]{0,1:T(8,128)(2,1)S(1)} collective-permute-done((bf16[128,28]{0,1:T(8,128)(2,1)S(1)}, bf16[128,28]{0,1:T(8,128)(2,1)S(1)}, u32[]{:S(2)}, u32[]{:S(2)}) %collective-permute-start.2) | collective-permute-done | bytes 7200 | tf_op jit(solution)/shard_map/ppermute | solution.py:172
  209.3 4.5 collective-permute-done.1
  213.9 6.0 %all_gather.12 = bf16[5,7,4096]{2,1,0:T(8,128)(2,1)S(1)} all-gather(bf16[5,7,2048]{2,1,0:T(8,128)(2,1)S(1)} %copy-done.11), channel_id=1, replica_groups=mesh['z'=4,'y'=2,'c'=2,'tensor'=2] {'tensor'}, dimensions={2}, use_global_device_ids=true | all-gather | bytes 430080 | tf_op jit(solution)/shard_map/all_gather | solution.py:238
  220.7 26.1 %collective-permute-done.6.refs_3_ = bf16[1280,1024]{1,0:T(8,128)(2,1)} collective-permute-done((bf16[1280,1024]{1,0:T(8,128)(2,1)S(1)}, bf16[1280,1024]{1,0:T(8,128)(2,1)}, u32[]{:S(2)}, u32[]{:S(2)}) %collective-permute-start.6) | collective-permute-done | bytes 2621472 | tf_op jit(solution)/shard_map/ppermute | solution.py:172
  247.4 4.6 all_gather.15
  252.5 2.3 collective-permute-start.3
  257.8 3.7 collective-permute-done.3
  263.7 12.3 %first_stage.1.refs_1_ = bf16[4,512,1024]{2,1,0:T(8,128)(2,1)} custom-call(bf16[512,28]{1,0:T(8,128)(2,1)} %copy.63.refs_0_, bf16[4,28,1024]{2,1,0:T(8,128)(2,1)} %pad_maximum_fusion.4.refs_1_, bf16[512,1280]{1,0:T(8,128)(2,1)} %pad_maximum_fusion.refs_2_, bf16[2,1280,1024]{2,1,0:T(8,128)(2,1)} %all-gather.5.cloned.1.call-done.refs_3_, f32[1,1024]{1,0:T(1,128)} %bitcast.209), custom_call_target="tpu_custom_call" | custom-call | flops 2684354560 | bytes 9437184 | tf_op jit(solution)/shard_map/first_stage/pallas_call | solution.py:98
  276.0 20.3 %mix.3 = bf16[4,4,128,1024]{3,2,1,0:T(8,128)(2,1)} custom-call(s32[4]{0:T(128)} %pad_add_fusion.refs_0_, bf16[4,512,1024]{2,1,0:T(8,128)(2,1)} %first_stage.1.refs_1_, bf16[1280,1024]{1,0:T(8,128)(2,1)} %get-tuple-element.56.refs_2_, bf16[1280,1024]{1,0:T(8,128)(2,1)} %collective-permute-done.12.refs_3_, bf16[1280,1024]{1,0:T(8,128)(2,1)} %collective-permute-done.13.refs_4_, ...), custom_call_target="tpu_custom_call" | custom-call | flops 15032385536 | bytes 14680064 | tf_op jit(solution)/shard_map/mix/pallas_call | solution.py:146
  296.3 2.9 slice_bitcast_fusion.7
  299.2 4.1 collective-permute-start.22
  303.3 20.2 %mix.2 = bf16[4,4,128,1024]{3,2,1,0:T(8,128)(2,1)} custom-call(s32[4]{0:T(128)} %pad_add_fusion.refs_0_, bf16[4,512,1024]{2,1,0:T(8,128)(2,1)} %first_stage.1.refs_1_, bf16[1280,1024]{1,0:T(8,128)(2,1)} %copy-done.4, bf16[1280,1024]{1,0:T(8,128)(2,1)} %collective-permute-done.6.refs_3_, bf16[1280,1024]{1,0:T(8,128)(2,1)} %collective-permute-done.7.refs_4_, ...), custom_call_target="tpu_custom_call" | custom-call | flops 15032385536 | bytes 14680064 | tf_op jit(solution)/shard_map/mix/pallas_call | solution.py:146
  323.6 2.6 slice_bitcast_fusion.10
  326.8 3.9 collective-permute-start.17
  330.7 3.8 collective-permute-start.19
  336.5 6.6 %collective-permute-done.9 = bf16[2,128,1024]{2,1,0:T(8,128)(2,1)S(1)} collective-permute-done((bf16[2,128,1024]{2,1,0:T(8,128)(2,1)}, bf16[2,128,1024]{2,1,0:T(8,128)(2,1)S(1)}, u32[]{:S(2)}, u32[]{:S(2)}) %collective-permute-start.9) | collective-permute-done | bytes 524320 | tf_op jit(solution)/shard_map/ppermute | solution.py:172
  343.1 11.5 %collective-permute-start.23 = (bf16[2,128,1024]{2,1,0:T(8,128)(2,1)S(1)}, bf16[2,128,1024]{2,1,0:T(8,128)(2,1)S(1)}, u32[]{:S(2)}, u32[]{:S(2)}) collective-permute-start(bf16[2,128,1024]{2,1,0:T(8,128)(2,1)S(1)} %get-tuple-element.72), channel_id=1, source_target_pairs={{0,24},{8,0},{16,8},{24,16},{1,25},{9,1},{17,9},{25,17},{2,26},{10... | collective-permute-start | bytes 1572872 | tf_op jit(solution)/shard_map/ppermute | solution.py:172
  354.5 22.3 %collective-permute-done.19 = bf16[2,128,1024]{2,1,0:T(8,128)(2,1)S(1)} collective-permute-done((bf16[2,128,1024]{2,1,0:T(8,128)(2,1)S(1)}, bf16[2,128,1024]{2,1,0:T(8,128)(2,1)S(1)}, u32[]{:S(2)}, u32[]{:S(2)}) %collective-permute-start.19) | collective-permute-done | bytes 524320 | tf_op jit(solution)/shard_map/ppermute | solution.py:172
  381.1 7.0 %collective-permute-done.16 = bf16[2,128,1024]{2,1,0:T(8,128)(2,1)S(1)} collective-permute-done((bf16[2,128,1024]{2,1,0:T(8,128)(2,1)S(1)}, bf16[2,128,1024]{2,1,0:T(8,128)(2,1)S(1)}, u32[]{:S(2)}, u32[]{:S(2)}) %collective-permute-start.16) | collective-permute-done | bytes 524320 | tf_op jit(solution)/shard_map/ppermute | solution.py:172
  388.1 22.6 %collective-permute-start.20 = (bf16[2,128,1024]{2,1,0:T(8,128)(2,1)S(1)}, bf16[2,128,1024]{2,1,0:T(8,128)(2,1)S(1)}, u32[]{:S(2)}, u32[]{:S(2)}) collective-permute-start(bf16[2,128,1024]{2,1,0:T(8,128)(2,1)S(1)} %get-tuple-element.64), channel_id=1, source_target_pairs={{0,24},{8,0},{16,8},{24,16},{1,25},{9,1},{17,9},{25,17},{2,26},{10... | collective-permute-start | bytes 1572872 | tf_op jit(solution)/shard_map/ppermute | solution.py:172
  413.2 8.7 %collective-permute-done.18 = bf16[2,128,1024]{2,1,0:T(8,128)(2,1)S(1)} collective-permute-done((bf16[2,128,1024]{2,1,0:T(8,128)(2,1)S(1)}, bf16[2,128,1024]{2,1,0:T(8,128)(2,1)S(1)}, u32[]{:S(2)}, u32[]{:S(2)}) %collective-permute-start.18) | collective-permute-done | bytes 524320 | tf_op jit(solution)/shard_map/ppermute | solution.py:172
  421.9 11.2 %collective-permute-done.10 = bf16[2,128,1024]{2,1,0:T(8,128)(2,1)S(1)} collective-permute-done((bf16[2,128,1024]{2,1,0:T(8,128)(2,1)S(1)}, bf16[2,128,1024]{2,1,0:T(8,128)(2,1)S(1)}, u32[]{:S(2)}, u32[]{:S(2)}) %collective-permute-start.10) | collective-permute-done | bytes 524320 | tf_op jit(solution)/shard_map/ppermute | solution.py:172
  433.1 7.0 %collective-permute-done.20 = bf16[2,128,1024]{2,1,0:T(8,128)(2,1)S(1)} collective-permute-done((bf16[2,128,1024]{2,1,0:T(8,128)(2,1)S(1)}, bf16[2,128,1024]{2,1,0:T(8,128)(2,1)S(1)}, u32[]{:S(2)}, u32[]{:S(2)}) %collective-permute-start.20) | collective-permute-done | bytes 524320 | tf_op jit(solution)/shard_map/ppermute | solution.py:172
  448.3 2.3 fusion.4
  450.6 2.3 fusion.5
  457.1 7.2 %psum.7 = f32[128,28]{0,1:T(8,128)S(1)} all-reduce(f32[128,28]{0,1:T(8,128)S(1)} %pad_maximum_fusion.6), channel_id=1, replica_groups=mesh['z'=4,'y'=2,'c'=2,'tensor'=2] {'tensor'}, use_global_device_ids=true, to_apply=%region_32.33 | all-reduce | flops 3584 | bytes 28672 | tf_op jit(solution)/shard_map/psum | solution.py:287
  (147 shorter events, 40.5 us)
Async XLA Ops:
  7.2 186.7 %copy-start = (bf16[1024,256]{1,0:T(8,128)(2,1)S(1)}, bf16[1024,256]{1,0:T(8,128)(2,1)}, u32[]{:S(2)}) copy-start(bf16[1024,256]{1,0:T(8,128)(2,1)} %param.18) | copy-start | bytes 1572868
  7.2 29.4 %all-gather.3.cloned.1.call-start = ((), (), s32[]{:S(2)}) async-start(), calls=%async_computation.1 | async-start | bytes 1966080 | tf_op jit(solution)/shard_map/all_gather | solution.py:235
  9.5 254.3 %all-gather.5.cloned.1.call-start = ((), (), s32[]{:S(2)}) async-start(), calls=%async_computation.2 | async-start | bytes 6553600 | tf_op jit(solution)/shard_map/all_gather | solution.py:237
  100.2 92.8 %copy-start.20 = (s32[128]{0:T(128)S(1)}, s32[128]{0:T(128)}, u32[]{:S(2)}) copy-start(s32[128]{0:T(128)} %param.14) | copy-start | bytes 1540
  104.8 115.7 %copy-start.4 = (bf16[1280,1024]{1,0:T(8,128)(2,1)}, bf16[1280,1024]{1,0:T(8,128)(2,1)S(1)}, u32[]{:S(2)}) copy-start(bf16[1280,1024]{1,0:T(8,128)(2,1)S(1)} %get-tuple-element.55.refs_2_) | copy-start | bytes 7864324
  104.8 88.1 %collective-permute-start.12 = (bf16[1280,1024]{1,0:T(8,128)(2,1)}, bf16[1280,1024]{1,0:T(8,128)(2,1)}, u32[]{:S(2)}, u32[]{:S(2)}) collective-permute-start(bf16[1280,1024]{1,0:T(8,128)(2,1)} %get-tuple-element.56.refs_2_), channel_id=1, source_target_pairs={{0,4},{4,0},{1,5},{5,1},{2,6},{6,2},{3,7},{7,3},{8,12},{12,8},{9,1... | collective-permute-start | bytes 7864328 | tf_op jit(solution)/shard_map/ppermute | solution.py:172
  106.3 140.5 %collective-permute-start.6 = (bf16[1280,1024]{1,0:T(8,128)(2,1)S(1)}, bf16[1280,1024]{1,0:T(8,128)(2,1)}, u32[]{:S(2)}, u32[]{:S(2)}) collective-permute-start(bf16[1280,1024]{1,0:T(8,128)(2,1)S(1)} %get-tuple-element.55.refs_2_), channel_id=1, source_target_pairs={{0,4},{4,0},{1,5},{5,1},{2,6},{6,2},{3,7},{7,3},{8,12},{12,8},{9,1... | collective-permute-start | bytes 7864328 | tf_op jit(solution)/shard_map/ppermute | solution.py:172
  106.8 169.2 %collective-permute-start.13 = (bf16[1280,1024]{1,0:T(8,128)(2,1)}, bf16[1280,1024]{1,0:T(8,128)(2,1)}, u32[]{:S(2)}, u32[]{:S(2)}) collective-permute-start(bf16[1280,1024]{1,0:T(8,128)(2,1)} %get-tuple-element.56.refs_2_), channel_id=1, source_target_pairs={{0,2},{2,0},{1,3},{3,1},{4,6},{6,4},{5,7},{7,5},{8,10},{10,8},{9,1... | collective-permute-start | bytes 7864328 | tf_op jit(solution)/shard_map/ppermute | solution.py:172
  193.0 83.1 %collective-permute-start.14 = (bf16[1280,1024]{1,0:T(8,128)(2,1)}, bf16[1280,1024]{1,0:T(8,128)(2,1)}, u32[]{:S(2)}, u32[]{:S(2)}) collective-permute-start(bf16[1280,1024]{1,0:T(8,128)(2,1)} %collective-permute-done.12.refs_3_), channel_id=1, source_target_pairs={{0,2},{2,0},{1,3},{3,1},{4,6},{6,4},{5,7},{7,5},{8,10},{10,8},{9,1... | collective-permute-start | bytes 7864328 | tf_op jit(solution)/shard_map/ppermute | solution.py:172
  195.5 18.3 %copy-start.11 = (bf16[5,7,2048]{2,1,0:T(8,128)(2,1)S(1)}, bf16[5,7,2048]{2,1,0:T(8,128)(2,1)}, u32[]{:S(2)}) copy-start(bf16[5,7,2048]{2,1,0:T(8,128)(2,1)} %param.20) | copy-start | bytes 430084
  197.1 23.4 %collective-permute-start.5 = (bf16[128,1280]{1,0:T(8,128)(2,1)S(1)}, bf16[128,1280]{1,0:T(8,128)(2,1)}, u32[]{:S(2)}, u32[]{:S(2)}) collective-permute-start(bf16[128,1280]{1,0:T(8,128)(2,1)S(1)} %copy.59), channel_id=1, source_target_pairs={{0,8},{8,16},{16,24},{24,0},{1,9},{9,17},{17,25},{25,1},{2,10},{10... | collective-permute-start | bytes 983048 | tf_op jit(solution)/shard_map/ppermute | solution.py:172
  197.4 22.5 %copy-start.14 = (bf16[128,28]{0,1:T(8,128)(2,1)}, bf16[128,28]{0,1:T(8,128)(2,1)S(1)}, u32[]{:S(2)}) copy-start(bf16[128,28]{0,1:T(8,128)(2,1)S(1)} %convert_element_type.223) | copy-start | bytes 21508
  197.4 11.9 %collective-permute-start.2 = (bf16[128,28]{0,1:T(8,128)(2,1)S(1)}, bf16[128,28]{0,1:T(8,128)(2,1)S(1)}, u32[]{:S(2)}, u32[]{:S(2)}) collective-permute-start(bf16[128,28]{0,1:T(8,128)(2,1)S(1)} %convert_element_type.223), channel_id=1, source_target_pairs={{0,8},{8,16},{16,24},{24,0},{1,9},{9,17},{17,25},{25,1},{2,10},{10... | collective-permute-start | bytes 21512 | tf_op jit(solution)/shard_map/ppermute | solution.py:172
  209.3 10.6 %copy-start.17 = (bf16[128,28]{0,1:T(8,128)(2,1)}, bf16[128,28]{0,1:T(8,128)(2,1)S(1)}, u32[]{:S(2)}) copy-start(bf16[128,28]{0,1:T(8,128)(2,1)S(1)} %collective-permute-done.2) | copy-start | bytes 21508
  209.3 4.5 collective-permute-start.1
  213.8 6.0 %collective-permute-start = (bf16[128,28]{0,1:T(8,128)(2,1)S(1)}, bf16[128,28]{0,1:T(8,128)(2,1)S(1)}, u32[]{:S(2)}, u32[]{:S(2)}) collective-permute-start(bf16[128,28]{0,1:T(8,128)(2,1)S(1)} %convert_element_type.223), channel_id=1, source_target_pairs={{0,24},{8,0},{16,8},{24,16},{1,25},{9,1},{17,9},{25,17},{2,26},{10... | collective-permute-start | bytes 21512 | tf_op jit(solution)/shard_map/ppermute | solution.py:172
  219.8 32.7 %collective-permute-start.4 = (bf16[128,1280]{1,0:T(8,128)(2,1)S(1)}, bf16[128,1280]{1,0:T(8,128)(2,1)}, u32[]{:S(2)}, u32[]{:S(2)}) collective-permute-start(bf16[128,1280]{1,0:T(8,128)(2,1)S(1)} %copy.59), channel_id=1, source_target_pairs={{0,16},{8,24},{16,0},{24,8},{1,17},{9,25},{17,1},{25,9},{2,18},{10... | collective-permute-start | bytes 983048 | tf_op jit(solution)/shard_map/ppermute | solution.py:172
  220.6 82.8 %collective-permute-start.7 = (bf16[1280,1024]{1,0:T(8,128)(2,1)S(1)}, bf16[1280,1024]{1,0:T(8,128)(2,1)}, u32[]{:S(2)}, u32[]{:S(2)}) collective-permute-start(bf16[1280,1024]{1,0:T(8,128)(2,1)S(1)} %get-tuple-element.55.refs_2_), channel_id=1, source_target_pairs={{0,2},{2,0},{1,3},{3,1},{4,6},{6,4},{5,7},{7,5},{8,10},{10,8},{9,1... | collective-permute-start | bytes 7864328 | tf_op jit(solution)/shard_map/ppermute | solution.py:172
  246.8 56.6 %collective-permute-start.8 = (bf16[1280,1024]{1,0:T(8,128)(2,1)}, bf16[1280,1024]{1,0:T(8,128)(2,1)}, u32[]{:S(2)}, u32[]{:S(2)}) collective-permute-start(bf16[1280,1024]{1,0:T(8,128)(2,1)} %collective-permute-done.6.refs_3_), channel_id=1, source_target_pairs={{0,2},{2,0},{1,3},{3,1},{4,6},{6,4},{5,7},{7,5},{8,10},{10,8},{9,1... | collective-permute-start | bytes 7864328 | tf_op jit(solution)/shard_map/ppermute | solution.py:172
  252.5 9.0 %collective-permute-start.3 = (bf16[128,1280]{1,0:T(8,128)(2,1)S(1)}, bf16[128,1280]{1,0:T(8,128)(2,1)S(1)}, u32[]{:S(2)}, u32[]{:S(2)}) collective-permute-start(bf16[128,1280]{1,0:T(8,128)(2,1)S(1)} %copy.59), channel_id=1, source_target_pairs={{0,24},{8,0},{16,8},{24,16},{1,25},{9,1},{17,9},{25,17},{2,26},{10... | collective-permute-start | bytes 983048 | tf_op jit(solution)/shard_map/ppermute | solution.py:172
  299.2 31.5 %collective-permute-start.15 = (bf16[2,128,1024]{2,1,0:T(8,128)(2,1)}, bf16[2,128,1024]{2,1,0:T(8,128)(2,1)}, u32[]{:S(2)}, u32[]{:S(2)}) collective-permute-start(bf16[2,128,1024]{2,1,0:T(8,128)(2,1)} %get-tuple-element.73), channel_id=1, source_target_pairs={{0,8},{8,16},{16,24},{24,0},{1,9},{9,17},{17,25},{25,1},{2,10},{10... | collective-permute-start | bytes 1572872 | tf_op jit(solution)/shard_map/ppermute | solution.py:172
  299.2 35.3 %collective-permute-start.22 = (bf16[2,128,1024]{2,1,0:T(8,128)(2,1)}, bf16[2,128,1024]{2,1,0:T(8,128)(2,1)}, u32[]{:S(2)}, u32[]{:S(2)}) collective-permute-start(bf16[2,128,1024]{2,1,0:T(8,128)(2,1)} %get-tuple-element.74), channel_id=1, source_target_pairs={{0,24},{8,0},{16,8},{24,16},{1,25},{9,1},{17,9},{25,17},{2,26},{10... | collective-permute-start | bytes 1572872 | tf_op jit(solution)/shard_map/ppermute | solution.py:172
  326.2 16.8 %collective-permute-start.9 = (bf16[2,128,1024]{2,1,0:T(8,128)(2,1)}, bf16[2,128,1024]{2,1,0:T(8,128)(2,1)S(1)}, u32[]{:S(2)}, u32[]{:S(2)}) collective-permute-start(bf16[2,128,1024]{2,1,0:T(8,128)(2,1)} %get-tuple-element.65), channel_id=1, source_target_pairs={{0,8},{8,16},{16,24},{24,0},{1,9},{9,17},{17,25},{25,1},{2,10},{10... | collective-permute-start | bytes 1572872 | tf_op jit(solution)/shard_map/ppermute | solution.py:172
  326.8 51.6 %collective-permute-start.17 = (bf16[2,128,1024]{2,1,0:T(8,128)(2,1)S(1)}, bf16[2,128,1024]{2,1,0:T(8,128)(2,1)S(1)}, u32[]{:S(2)}, u32[]{:S(2)}) collective-permute-start(bf16[2,128,1024]{2,1,0:T(8,128)(2,1)S(1)} %copy-done.6), channel_id=1, source_target_pairs={{0,24},{8,0},{16,8},{24,16},{1,25},{9,1},{17,9},{25,17},{2,26},{10... | collective-permute-start | bytes 1572872 | tf_op jit(solution)/shard_map/ppermute | solution.py:172
  330.7 49.8 %collective-permute-start.21 = (bf16[2,128,1024]{2,1,0:T(8,128)(2,1)S(1)}, bf16[2,128,1024]{2,1,0:T(8,128)(2,1)S(1)}, u32[]{:S(2)}, u32[]{:S(2)}) collective-permute-start(bf16[2,128,1024]{2,1,0:T(8,128)(2,1)S(1)} %copy-done.5), channel_id=1, source_target_pairs={{0,8},{8,16},{16,24},{24,0},{1,9},{9,17},{17,25},{25,1},{2,10},{10... | collective-permute-start | bytes 1572872 | tf_op jit(solution)/shard_map/ppermute | solution.py:172
  330.7 46.1 %collective-permute-start.19 = (bf16[2,128,1024]{2,1,0:T(8,128)(2,1)S(1)}, bf16[2,128,1024]{2,1,0:T(8,128)(2,1)S(1)}, u32[]{:S(2)}, u32[]{:S(2)}) collective-permute-start(bf16[2,128,1024]{2,1,0:T(8,128)(2,1)S(1)} %get-tuple-element.66), channel_id=1, source_target_pairs={{0,24},{8,0},{16,8},{24,16},{1,25},{9,1},{17,9},{25,17},{2,26},{10... | collective-permute-start | bytes 1572872 | tf_op jit(solution)/shard_map/ppermute | solution.py:172
  336.4 51.7 %collective-permute-start.16 = (bf16[2,128,1024]{2,1,0:T(8,128)(2,1)S(1)}, bf16[2,128,1024]{2,1,0:T(8,128)(2,1)S(1)}, u32[]{:S(2)}, u32[]{:S(2)}) collective-permute-start(bf16[2,128,1024]{2,1,0:T(8,128)(2,1)S(1)} %get-tuple-element.71), channel_id=1, source_target_pairs={{0,8},{8,16},{16,24},{24,0},{1,9},{9,17},{17,25},{25,1},{2,10},{10... | collective-permute-start | bytes 1572872 | tf_op jit(solution)/shard_map/ppermute | solution.py:172
  343.1 67.6 %collective-permute-start.23 = (bf16[2,128,1024]{2,1,0:T(8,128)(2,1)S(1)}, bf16[2,128,1024]{2,1,0:T(8,128)(2,1)S(1)}, u32[]{:S(2)}, u32[]{:S(2)}) collective-permute-start(bf16[2,128,1024]{2,1,0:T(8,128)(2,1)S(1)} %get-tuple-element.72), channel_id=1, source_target_pairs={{0,24},{8,0},{16,8},{24,16},{1,25},{9,1},{17,9},{25,17},{2,26},{10... | collective-permute-start | bytes 1572872 | tf_op jit(solution)/shard_map/ppermute | solution.py:172
  376.8 36.3 %collective-permute-start.11 = (bf16[2,128,1024]{2,1,0:T(8,128)(2,1)S(1)}, bf16[2,128,1024]{2,1,0:T(8,128)(2,1)S(1)}, u32[]{:S(2)}, u32[]{:S(2)}) collective-permute-start(bf16[2,128,1024]{2,1,0:T(8,128)(2,1)S(1)} %get-tuple-element.68), channel_id=1, source_target_pairs={{0,24},{8,0},{16,8},{24,16},{1,25},{9,1},{17,9},{25,17},{2,26},{10... | collective-permute-start | bytes 1572872 | tf_op jit(solution)/shard_map/ppermute | solution.py:172
  378.5 43.4 %collective-permute-start.18 = (bf16[2,128,1024]{2,1,0:T(8,128)(2,1)S(1)}, bf16[2,128,1024]{2,1,0:T(8,128)(2,1)S(1)}, u32[]{:S(2)}, u32[]{:S(2)}) collective-permute-start(bf16[2,128,1024]{2,1,0:T(8,128)(2,1)S(1)} %get-tuple-element.67), channel_id=1, source_target_pairs={{0,8},{8,16},{16,24},{24,0},{1,9},{9,17},{17,25},{25,1},{2,10},{10... | collective-permute-start | bytes 1572872 | tf_op jit(solution)/shard_map/ppermute | solution.py:172
  380.5 52.6 %collective-permute-start.10 = (bf16[2,128,1024]{2,1,0:T(8,128)(2,1)S(1)}, bf16[2,128,1024]{2,1,0:T(8,128)(2,1)S(1)}, u32[]{:S(2)}, u32[]{:S(2)}) collective-permute-start(bf16[2,128,1024]{2,1,0:T(8,128)(2,1)S(1)} %get-tuple-element.63), channel_id=1, source_target_pairs={{0,8},{8,16},{16,24},{24,0},{1,9},{9,17},{17,25},{25,1},{2,10},{10... | collective-permute-start | bytes 1572872 | tf_op jit(solution)/shard_map/ppermute | solution.py:172
  388.1 52.0 %collective-permute-start.20 = (bf16[2,128,1024]{2,1,0:T(8,128)(2,1)S(1)}, bf16[2,128,1024]{2,1,0:T(8,128)(2,1)S(1)}, u32[]{:S(2)}, u32[]{:S(2)}) collective-permute-start(bf16[2,128,1024]{2,1,0:T(8,128)(2,1)S(1)} %get-tuple-element.64), channel_id=1, source_target_pairs={{0,24},{8,0},{16,8},{24,16},{1,25},{9,1},{17,9},{25,17},{2,26},{10... | collective-permute-start | bytes 1572872 | tf_op jit(solution)/shard_map/ppermute | solution.py:172
  (20 other events, 77.7 us)
Sparse Core Ops, SparseCore 0:
  9.6 26.9 all-gather.2
  100.3 66.7 all-gather.4
where the time goes:
time: 473 us; the launch traced here: 472 us
  waiting for transfers between devices  220 us (47%)
  blocking collectives  70.3 us (15%)
  starting transfers between devices  53.9 us (11%)
  Pallas kernels  52.8 us (11%)
  local copies, waits for them, and re-layouts  32.6 us (7%)
  other arithmetic  17.7 us (4%)
  between operations  14.6 us (3%)
  matrix products  10.2 us (2%)
    ppermute x24, waiting for transfers between devices, hop(): lax.ppermute(value, axis, [(i, (i + step) % size) for i in range(size)])  193 us
    ppermute x24, starting transfers between devices, hop(): lax.ppermute(value, axis, [(i, (i + step) % size) for i in range(size)])  53.8 us
    all_to_all x1, blocking collectives, body(): film = lax.all_to_all(film, 'z', split_axis=2, concat_axis=1, tiled=True)  52.5 us
    pallas_call x2, Pallas kernels, mix(): pl.pallas_call(kern, grid=(width // nt,), in_specs=[pl.BlockSpec(memory_s...  40.5 us
    all_gather x1, waiting for transfers between devices, body(): film = lax.all_gather(film, 'tensor', axis=2, tiled=True)  27.1 us
    pallas_call x1, Pallas kernels, first_stage(): pl.pallas_call(kern, grid=(width // gw, rows // rt), in_specs=[pl.BlockSp...  12.3 us
  transfers between devices with their start and end apart: 26, of which 12 were waited for; matrix products, arithmetic and copies ran while one was open for 6% of the time, Pallas kernels for 11%

commit v1 on v0

--- a/solution.py
+++ b/solution.py
@@ -199,7 +199,7 @@
     return out
 
 
-def body(
+def general_body(
     noisy_sample,
     timestep,
     noise,
@@ -289,8 +289,610 @@
     return (eps, denoised)
 
 
+CHUNK = 256
+SPLIT = 2
+LANES = 128
+MESH_ID = pl.DeviceIdType.MESH
+
+
+def remote(src, dst, send, recv, where):
+    return pltpu.make_async_remote_copy(
+        src_ref=src,
+        dst_ref=dst,
+        send_sem=send,
+        recv_sem=recv,
+        device_id=where,
+        device_id_type=MESH_ID,
+    )
+
+
+def normed(hs, gain):
+    count = len(hs) * hs[0].shape[1]
+    mean = sum(jnp.sum(h, axis=1, keepdims=True) for h in hs) / count
+    hs = [h - mean for h in hs]
+    var = sum(jnp.sum(h * h, axis=1, keepdims=True) for h in hs) / count
+    inv = 1.0 / jnp.sqrt(var + 1e-05)
+    return [h * inv * gain for h in hs]
+
+
+def fused_kernel(
+    sinus_ref,
+    obs_ref,
+    samp_ref,
+    w1_ref,
+    w2_ref,
+    film_ref,
+    toep_ref,
+    gain_one_ref,
+    mid_ref,
+    res_ref,
+    outw_ref,
+    gain_two_ref,
+    eps_ref,
+    w_buf,
+    a_buf,
+    film_buf,
+    cond_buf,
+    toep_buf,
+    gain_buf,
+    own_part,
+    z_recv,
+    z_send,
+    last,
+    eps_acc,
+    eps_send,
+    eps_recv,
+    own_sem,
+    core_send,
+    core_recv,
+    y_send,
+    y_recv,
+    fwd_send,
+    fwd_recv,
+    film_send,
+    film_recv,
+    filmy_sem,
+    filmx_send,
+    filmx_recv,
+    filmc_send,
+    filmc_recv,
+    toep_send,
+    toep_recv,
+    cond_send,
+    cond_recv,
+    condx_send,
+    condx_recv,
+    zs_sem,
+    zr_sem,
+    eps_ssem,
+    eps_rsem,
+):
+    zi, yi = lax.axis_index("z"), lax.axis_index("y")
+    ci, xi = lax.axis_index("c"), lax.axis_index("tensor")
+    zn = DEPTH_PARTS
+    f32, b16 = jnp.float32, jnp.bfloat16
+    chunks = w_buf.shape[0]
+    cl = w_buf.shape[2] // TAPS
+    rows = eps_ref.shape[0]
+    gw = C // GROUPS
+    width = mid_ref.shape[1]
+    kw = film_buf.shape[5]
+    feat = w2_ref.shape[1] + obs_ref.shape[1]
+    mid = TAPS // 2
+    oy, oc, ox = 1 - yi, 1 - ci, 1 - xi
+    to_y, to_c, to_x = {"y": oy}, {"c": oc}, {"tensor": ox}
+
+    barrier = pltpu.get_barrier_semaphore()
+    peers = [to_y, to_c]
+    for dz in range(zn):
+        for dx in range(2):
+            if dz or dx:
+                peers.append({"z": lax.rem(zi + dz, zn), "tensor": lax.rem(xi + dx, 2)})
+    for peer in peers:
+        pl.semaphore_signal(barrier, inc=1, device_id=peer, device_id_type=MESH_ID)
+
+    def cols(j):
+        return pl.ds(pl.multiple_of(j * CHUNK, CHUNK), CHUNK)
+
+    def own_copy(j):
+        return pltpu.make_async_copy(mid_ref.at[:, cols(j)], w_buf.at[j, 0], own_sem.at[j])
+
+    def core_copy(j):
+        return remote(
+            mid_ref.at[:, cols(j)], w_buf.at[j, 1], core_send.at[j], core_recv.at[j], to_c
+        )
+
+    def y_copy(j):
+        return remote(mid_ref.at[:, cols(j)], w_buf.at[j, 2], y_send.at[j], y_recv.at[j], to_y)
+
+    def fwd_copy(j):
+        return remote(w_buf.at[j, 2], w_buf.at[j, 3], fwd_send.at[j], fwd_recv.at[j], to_c)
+
+    def film_out(q, t):
+        return remote(
+            film_ref.at[t, :, pl.ds(q * kw, kw)],
+            film_buf.at[t, zi, yi, ci],
+            film_send.at[q, t],
+            film_recv.at[zi],
+            {"z": 2 * xi + q, "tensor": t},
+        )
+
+    pl.semaphore_wait(barrier, len(peers))
+    y_copy(0).start()
+    for q in range(2):
+        for t in range(2):
+            mine = (2 * xi + q == zi) & (xi == t)
+
+            @pl.when(mine)
+            def _():
+                pltpu.make_async_copy(
+                    film_ref.at[t, :, pl.ds(q * kw, kw)],
+                    film_buf.at[t, zi, yi, ci],
+                    film_recv.at[zi],
+                ).start()
+
+            @pl.when(jnp.logical_not(mine))
+            def _():
+                film_out(q, t).start()
+
+    home = zi // 2
+    at = pl.ds(pl.multiple_of(lax.rem(zi, 2) * kw, kw), kw)
+
+    def toep_copy():
+        return remote(
+            toep_ref.at[:, :, at], toep_buf, toep_send.at[0], toep_recv.at[0], to_x
+        )
+
+    def gain_copy():
+        return remote(gain_one_ref.at[:, at], gain_buf, toep_send.at[1], toep_recv.at[1], to_x)
+
+    @pl.when(xi == home)
+    def _():
+        toep_copy().start()
+        gain_copy().start()
+        pltpu.make_async_copy(toep_ref.at[:, :, at], toep_buf, toep_recv.at[0]).start()
+        pltpu.make_async_copy(gain_one_ref.at[:, at], gain_buf, toep_recv.at[1]).start()
+
+    hidden = mish(jnp.dot(sinus_ref[...], w1_ref[...], preferred_element_type=f32)).astype(b16)
+    step_feat = jnp.dot(hidden, w2_ref[...], preferred_element_type=f32)
+    half = rows // 2
+    sw = step_feat.shape[1]
+    cond_step = mish(step_feat).astype(b16)
+    cond_obs = mish(obs_ref[...].astype(f32)).astype(b16)
+    for i in range(2):
+        part = slice(i * half, (i + 1) * half)
+        cond_buf[zi, i, :, :sw] = cond_step[part]
+        cond_buf[zi, i, :, sw:feat] = cond_obs[part]
+        cond_buf[zi, i, :, feat:] = samp_ref[part]
+
+    def cond_copy(dz):
+        return remote(
+            cond_buf.at[zi, xi],
+            cond_buf.at[zi, xi],
+            cond_send.at[dz - 1],
+            cond_recv.at[zi],
+            {"z": lax.rem(zi + dz, zn)},
+        )
+
+    def condx_copy(z, i):
+        return remote(
+            cond_buf.at[z, i], cond_buf.at[z, i], condx_send.at[z], condx_recv.at[z], to_x
+        )
+
+    def cond_in(z):
+        return remote(
+            cond_buf.at[z, xi], cond_buf.at[z, xi], cond_send.at[0], cond_recv.at[z], to_x
+        )
+
+    for dz in range(1, zn):
+        cond_copy(dz).start()
+
+    @pl.loop(0, chunks)
+    def _(j):
+        own_copy(j).start()
+        core_copy(j).start()
+
+    def film_x(i, t, y):
+        piece = film_buf.at[t, :, y, ci]
+        return remote(piece, piece, filmx_send.at[i], filmx_recv.at[i], to_x)
+
+    def film_y(y):
+        piece = film_buf.at[xi, :, y, ci]
+        return remote(piece, piece, filmy_sem.at[0], filmy_sem.at[1], to_y)
+
+    def film_c(i, t, y, c):
+        piece = film_buf.at[t, :, y, c]
+        return remote(piece, piece, filmc_send.at[i], filmc_recv.at[i], to_c)
+
+    for z in range(zn):
+        piece = film_buf.at[xi, z, yi, ci]
+        remote(piece, piece, film_send.at[0, 0], film_recv.at[z], to_x).wait_recv()
+    film_y(yi).start()
+    film_x(0, xi, yi).start()
+    film_c(0, xi, yi, ci).start()
+
+    @pl.loop(1, chunks)
+    def _(j):
+        y_copy(j).start()
+
+    for dz in range(1, zn):
+        z = lax.rem(zi + dz, zn)
+        cond_in(z).wait_recv()
+        condx_copy(z, xi).start()
+    film_y(oy).wait_recv()
+    film_x(1, xi, oy).start()
+    film_c(1, xi, oy, ci).start()
+    film_x(0, ox, yi).wait_recv()
+    film_c(2, ox, yi, ci).start()
+    film_x(1, ox, oy).wait_recv()
+    film_c(3, ox, oy, ci).start()
+    toep_copy().wait_recv()
+    gain_copy().wait_recv()
+    for dz in range(1, zn):
+        condx_copy(lax.rem(zi + dz, zn), ox).wait_recv()
+    for i, (t, y) in enumerate(((xi, yi), (xi, oy), (ox, yi), (ox, oy))):
+        film_c(i, t, y, oc).wait_recv()
+
+    per = gw // cl
+    inner = film_buf.shape[1] * film_buf.shape[2] * film_buf.shape[3] * film_buf.shape[4]
+
+    @pl.loop(0, zn)
+    def _(z):
+        cond = cond_buf[z].reshape(rows, cond_buf.shape[3])
+        x = cond[:, feat : feat + toep_buf.shape[1]]
+        cond = cond[:, :feat]
+        ab = z // SPLIT
+        r = lax.rem(z, SPLIT)
+        for g in range(kw // gw):
+            span = slice(g * gw, (g + 1) * gw)
+            hs = [
+                jnp.dot(x, toep_buf[h, :, span], preferred_element_type=f32)
+                for h in range(HORIZON)
+            ]
+            hs = normed(hs, gain_buf[0:1, span])
+            scale = jnp.dot(
+                cond,
+                film_buf[0, :, :, :, :, span].reshape(inner, gw),
+                preferred_element_type=f32,
+            )
+            shift = jnp.dot(
+                cond,
+                film_buf[1, :, :, :, :, span].reshape(inner, gw),
+                preferred_element_type=f32,
+            )
+            for h in range(HORIZON):
+                val = (scale * mish(hs[h]) + shift).astype(b16)
+                for b in range(per):
+                    a_buf[g * per + b, r, ab, :, h * cl : (h + 1) * cl] = val[
+                        :, b * cl : (b + 1) * cl
+                    ]
+
+    eps_acc[...] = jnp.zeros_like(eps_acc)
+    order = [yi * 2 + ci, yi * 2 + oc, oy * 2 + ci, oy * 2 + oc]
+    steps = chunks * SPLIT
+    ring = own_part.shape[0]
+    ends = (zi == 0) | (zi == zn - 1)
+
+    def z_copy(d, s):
+        k = lax.rem(s, ring)
+        return remote(
+            z_send.at[d, k],
+            z_recv.at[d, s],
+            zs_sem.at[d, k],
+            zr_sem.at[d, s],
+            {"z": jnp.maximum(zi - 1, 0) if d == 0 else jnp.minimum(zi + 1, zn - 1)},
+        )
+
+    def flow(d, now):
+        lag = zn - 1 - zi if d == 0 else zi
+        s = now - lag
+        k = lax.rem(s + ring, ring)
+
+        @pl.when((s >= 0) & (s < steps))
+        def _():
+            @pl.when(lag > 0)
+            def _():
+                z_copy(d, s).wait_recv()
+
+            @pl.when(lag == zn - 1)
+            def _():
+                for h in range(HORIZON):
+                    last[lax.rem(s, SPLIT), lax.rem(s // SPLIT, 2), h] = own_part[
+                        k, d, h
+                    ] + z_recv[d, s, h].astype(f32)
+
+            @pl.when(lag < zn - 1)
+            def _():
+                @pl.when(s >= ring)
+                def _():
+                    z_copy(d, s - ring).wait_send()
+
+                @pl.when(lag == 0)
+                def _():
+                    for h in range(HORIZON):
+                        z_send[d, k, h] = own_part[k, d, h].astype(b16)
+
+                @pl.when(lag > 0)
+                def _():
+                    for h in range(HORIZON):
+                        z_send[d, k, h] = (
+                            own_part[k, d, h] + z_recv[d, s, h].astype(f32)
+                        ).astype(b16)
+
+                z_copy(d, s).start()
+
+    @pl.loop(0, steps + zn - 1)
+    def _(now):
+        @pl.when(now < steps)
+        def _():
+            j = now // SPLIT
+            r = lax.rem(now, SPLIT)
+            k = lax.rem(now, ring)
+
+            @pl.when(r == 0)
+            def _():
+                y_copy(j).wait_recv()
+                fwd_copy(j).start()
+                own_copy(j).wait()
+                core_copy(j).wait_recv()
+                fwd_copy(j).wait_recv()
+
+            for h in range(HORIZON):
+                p0 = max(0, h - mid)
+                p1 = min(HORIZON, h - mid + TAPS)
+                k0 = p0 - h + mid
+                k1 = p1 - h + mid
+                acc = None
+                for slot in range(4):
+                    left = a_buf[order[slot], r, :, :, p0 * cl : p1 * cl]
+                    term = jnp.dot(
+                        left.reshape(2 * rows, (p1 - p0) * cl),
+                        w_buf[j, slot, k0 * cl : k1 * cl, :],
+                        preferred_element_type=f32,
+                    )
+                    acc = term if acc is None else acc + term
+                for d in range(2):
+                    own_part[k, d, h] = acc[d * rows : (d + 1) * rows]
+
+        flow(1, now)
+        flow(0, now)
+        done = now - (zn - 1)
+
+        @pl.when((done >= 0) & ends & (lax.rem(done // SPLIT, 2) == 1))
+        def _():
+            r = lax.rem(done, SPLIT)
+            g = done // (2 * SPLIT)
+            z = (zi // (zn - 1)) * SPLIT + r
+            span = pl.ds(pl.multiple_of(g * gw, gw), gw)
+            hs = [
+                jnp.concatenate([last[r, 0, h], last[r, 1, h]], axis=1) for h in range(HORIZON)
+            ]
+            hs = normed(hs, gain_two_ref[0:1, span])
+            x = cond_buf[z, :, :, feat:].reshape(rows, LANES)[:, : res_ref.shape[1]]
+            for h in range(HORIZON):
+                skip = jnp.dot(x, res_ref[h, :, span], preferred_element_type=f32)
+                act = (mish(hs[h]) + skip).astype(b16)
+                eps_acc[r, h] += jnp.dot(act, outw_ref[span, :], preferred_element_type=f32)
+
+    end = (zi // SPLIT) * (zn - 1)
+
+    def eps_copy(r, t):
+        return remote(
+            eps_send.at[r],
+            eps_recv.at[xi],
+            eps_ssem.at[r, t],
+            eps_rsem.at[xi],
+            {"z": (zi // (zn - 1)) * SPLIT + r, "tensor": t},
+        )
+
+    for r in range(SPLIT):
+        z = (zi // (zn - 1)) * SPLIT + r
+
+        @pl.when(ends)
+        def _():
+            total = eps_acc[r, 0]
+            for h in range(1, HORIZON):
+                total = total + pltpu.roll(eps_acc[r, h], h * ACT, 1)
+            eps_send[r] = total
+
+            @pl.when(z == zi)
+            def _():
+                eps_recv[xi] = total
+
+            for t in range(2):
+
+                @pl.when((z != zi) | (xi != t))
+                def _():
+                    eps_copy(r, t).start()
+
+    for t in range(2):
+
+        @pl.when((zi != end) | (xi != t))
+        def _():
+            remote(
+                eps_send.at[0], eps_recv.at[t], eps_ssem.at[0, 0], eps_rsem.at[t], to_x
+            ).wait_recv()
+
+    eps_ref[...] = eps_recv[0] + eps_recv[1]
+
+    for r in range(SPLIT):
+        z = (zi // (zn - 1)) * SPLIT + r
+        for t in range(2):
+
+            @pl.when(ends & ((z != zi) | (xi != t)))
+            def _():
+                eps_copy(r, t).wait_send()
+
+    for d in range(2):
+
+        @pl.when((zi < zn - 1) if d else (zi > 0))
+        def _():
+            for s in range(steps - ring, steps):
+                z_copy(d, s).wait_send()
+
+    @pl.loop(0, chunks)
+    def _(j):
+        y_copy(j).wait_send()
+        core_copy(j).wait_send()
+        fwd_copy(j).wait_send()
+
+    for q in range(2):
+        for t in range(2):
+
+            @pl.when((2 * xi + q != zi) | (xi != t))
+            def _():
+                film_out(q, t).wait_send()
+
+    @pl.when(xi == home)
+    def _():
+        toep_copy().wait_send()
+        gain_copy().wait_send()
+
+    for dz in range(1, zn):
+        cond_copy(dz).wait_send()
+        condx_copy(lax.rem(zi + dz, zn), xi).wait_send()
+    film_y(yi).wait_send()
+    film_x(0, xi, yi).wait_send()
+    film_x(1, xi, oy).wait_send()
+    for i, (t, y) in enumerate(((xi, yi), (xi, oy), (ox, yi), (ox, oy))):
+        film_c(i, t, y, ci).wait_send()
+
+
+def fused(sinus, obs, samp, w1, w2, film, toep, gain_one, weights, res, outw, gain_two):
+    rows = obs.shape[0]
+    depth, width = weights.shape
+    chunks = width // CHUNK
+    cl = depth // TAPS
+    kw = cl * 4
+    fr = film.shape[1]
+    feat = w2.shape[1] + obs.shape[1]
+    steps = chunks * SPLIT
+    ring = DEPTH_PARTS
+    b16, f32 = jnp.bfloat16, jnp.float32
+    dma = pltpu.SemaphoreType.DMA
+    vm = pl.BlockSpec(memory_space=pltpu.VMEM)
+    hbm = pl.BlockSpec(memory_space=pl.ANY)
+    return pl.pallas_call(
+        fused_kernel,
+        out_shape=jax.ShapeDtypeStruct((rows, LANES), f32),
+        in_specs=[vm, vm, vm, vm, vm, hbm, hbm, hbm, hbm, vm, vm, vm],
+        out_specs=vm,
+        scratch_shapes=[
+            pltpu.VMEM((chunks, 4, depth, CHUNK), b16),
+            pltpu.VMEM((4, SPLIT, 2, rows, HORIZON * cl), b16),
+            pltpu.VMEM((2, DEPTH_PARTS, 2, 2, fr, kw), b16),
+            pltpu.VMEM((DEPTH_PARTS, 2, rows // 2, feat + LANES), b16),
+            pltpu.VMEM((HORIZON, toep.shape[1], kw), b16),
+            pltpu.VMEM((gain_one.shape[0], kw), f32),
+            pltpu.VMEM((ring, 2, HORIZON, rows, CHUNK), f32),
+            pltpu.VMEM((2, steps, HORIZON, rows, CHUNK), b16),
+            pltpu.VMEM((2, ring, HORIZON, rows, CHUNK), b16),
+            pltpu.VMEM((SPLIT, 2, HORIZON, rows, CHUNK), f32),
+            pltpu.VMEM((SPLIT, HORIZON, rows, LANES), f32),
+            pltpu.VMEM((SPLIT, rows, LANES), f32),
+            pltpu.VMEM((2, rows, LANES), f32),
+            dma((chunks,)),
+            dma((chunks,)),
+            dma((chunks,)),
+            dma((chunks,)),
+            dma((chunks,)),
+            dma((chunks,)),
+            dma((chunks,)),
+            dma((2, 2)),
+            dma((DEPTH_PARTS,)),
+            dma((2,)),
+            dma((2,)),
+            dma((2,)),
+            dma((4,)),
+            dma((4,)),
+            dma((2,)),
+            dma((2,)),
+            dma((DEPTH_PARTS - 1,)),
+            dma((DEPTH_PARTS,)),
+            dma((DEPTH_PARTS,)),
+            dma((DEPTH_PARTS,)),
+            dma((2, ring)),
+            dma((2, steps)),
+            dma((SPLIT, 2)),
+            dma((2,)),
+        ],
+        compiler_params=pltpu.CompilerParams(
+            collective_id=0, has_side_effects=True, vmem_limit_bytes=VMEM
+        ),
+        name="fused_step",
+    )(sinus, obs, samp, w1, w2, film, toep, gain_one, weights, res, outw, gain_two)
+
+
+def spread(blocks, lead):
+    width = next(b for b in blocks if b is not None).shape[1]
+    rows = []
+    for p in range(HORIZON):
+        rows.append(blocks[p] if blocks[p] is not None else jnp.zeros((ACT, width), lead))
+    rows.append(jnp.zeros((32 - HORIZON * ACT, width), lead))
+    return jnp.concatenate(rows, axis=0)
+
+
+def fused_body(
+    noisy_sample,
+    timestep,
+    noise,
+    obs_feat,
+    step_w1,
+    step_w2,
+    film_weight,
+    conv_in_w,
+    residual_w,
+    conv_mid_w,
+    out_w,
+    gain_one,
+    gain_two,
+):
+    width = conv_in_w.shape[2]
+    lead = conv_in_w.dtype
+    taps = lambda h, p: p - h + TAPS // 2
+    toep = jnp.stack(
+        [
+            spread(
+                [
+                    conv_in_w[taps(h, p)] if 0 <= taps(h, p) < TAPS else None
+                    for p in range(HORIZON)
+                ],
+                lead,
+            )
+            for h in range(HORIZON)
+        ]
+    )
+    blank = jnp.zeros((ACT, width), lead)
+    res = jnp.stack(
+        [
+            spread([residual_w if p == h else blank for p in range(HORIZON)], lead)
+            for h in range(HORIZON)
+        ]
+    )
+    samp = jnp.pad(
+        noisy_sample.astype(lead), ((0, 0), (0, LANES - noisy_sample.shape[1]))
+    )
+    eps = fused(
+        sinusoid(timestep).astype(lead),
+        obs_feat,
+        samp,
+        step_w1,
+        step_w2,
+        jnp.transpose(film_weight, (1, 0, 2)),
+        toep,
+        jnp.broadcast_to(gain_one[None, :], (8, width)),
+        conv_mid_w.reshape(-1, width),
+        res,
+        jnp.pad(out_w, ((0, 0), (0, LANES - ACT))),
+        gain_two[None, :],
+    )[:, : HORIZON * ACT]
+    return (eps, denoise_step(noisy_sample, eps, noise, timestep))
+
+
 def solution(mesh):
     dp, tensor = mesh.shape["dp"], mesh.shape["tensor"]
+    near = dp // DEPTH_PARTS // 2
+    body = fused_body if near == 2 and tensor == 2 else general_body
     grid = Mesh(
         mesh.devices.reshape(DEPTH_PARTS, dp // DEPTH_PARTS // 2, 2, tensor),
         ("z", "y", "c", "tensor"),

time: 473 us -> 242 us (0.51)
  waiting for transfers between devices: 220 us -> 0 us
  Pallas kernels: 52.8 us -> 226 us
  blocking collectives: 70.3 us -> 0 us
  starting transfers between devices: 53.9 us -> 0 us
  local copies, waits for them, and re-layouts: 32.6 us -> 8.92 us
  between operations: 14.6 us -> 0.76 us
  other arithmetic: 17.7 us -> 5.39 us
  matrix products: 10.2 us -> 0 us
    ppermute x24 -> x0, waiting for transfers between devices: 193 us -> none  [hop(): lax.ppermute(value, axis, [(i, (i + step) % size) for i in range(size)])]
    pallas_call x3 -> x1, Pallas kernels: 52.8 us -> 226 us  [fused(): pl.pallas_call(fused_kernel, out_shape=jax.ShapeDtypeStruct((rows, LANES)...]
    ppermute x24 -> x0, starting transfers between devices: 53.8 us -> none  [hop(): lax.ppermute(value, axis, [(i, (i + step) % size) for i in range(size)])]
    all_to_all x1 -> x0, blocking collectives: 52.5 us -> none  [body(): film = lax.all_to_all(film, 'z', split_axis=2, concat_axis=1, tiled=True)]
    all_gather x2 -> x0, waiting for transfers between devices: 27.1 us -> none  [the longest x1 27.1 us: body(): film = lax.all_gather(film, 'tensor', axis=2, tiled=True)]
    all_gather x2 -> x0, blocking collectives: 10.5 us -> none  [the longest x1 5.99 us: body(): win = lax.all_gather(conv_in_w, 'tensor', axis=2, tiled=True)]
    dot_general x5 -> x0, matrix products: 10.2 us -> none  [the longest x4 8.52 us: body(): outs.append(jnp.dot(act_two, out_w, preferred_element_type=jnp.float32))]
    slice x3 -> x0, local copies, waits for them, and re-layouts: 10.1 us -> none  [the longest x2 5.56 us: reduce_parts(): up = hop(far[:half], 'z', 1)]
  transfers between devices with their start and end apart: 26 -> 0, of which waited for: 12 -> 0; matrix products, arithmetic and copies ran while one was open for 6% -> 0% of each run, Pallas kernels for 11% -> 0%
where the time goes in v1:
time: 242 us
  Pallas kernels  226 us (93%)
  local copies, waits for them, and re-layouts  8.92 us (4%)
  other arithmetic  5.39 us (2%)
    pallas_call x1, Pallas kernels, fused(): pl.pallas_call(fused_kernel, out_shape=jax.ShapeDtypeStruct((rows, LANES)...  226 us

profile of v1, /device:TPU:0, one launch (start us, length us, event | category | flops | bytes accessed | tf_op | source)
XLA Modules:
  0.0 241.5 jit_solution(11658014119743011442)
XLA Ops:
  0.6 0.0 copy-start
  0.6 0.0 copy-start.1
  0.7 0.0 copy-start.3
  0.7 0.9 slice_bitcast_fusion.2
  1.6 0.5 concatenate.30
  2.0 0.5 concatenate.31
  2.5 0.5 concatenate.29
  3.0 0.5 concatenate.32
  3.5 1.1 fusion
  4.5 1.1 pad_maximum_fusion
  5.7 0.7 add_maximum_fusion
  6.4 0.3 fusion.4
  6.7 0.6 pad_maximum_fusion.6.sinus_ref
  7.4 1.1 copy.44
  8.5 0.9 pad.9.outw_ref
  9.4 0.0 copy-done
  9.4 1.0 copy.53
  10.4 0.0 copy-done.1
  10.4 0.1 copy.42
  10.6 0.6 pad.8.samp_ref
  11.2 0.6 broadcast_in_dim.7.gain_one_ref
  11.8 226.5 %fused_step.1 = f32[128,128]{1,0:T(8,128)} custom-call(bf16[128,256]{1,0:T(8,128)(2,1)} %pad_maximum_fusion.6.sinus_ref, bf16[128,1024]{1,0:T(8,128)(2,1)} %obs_ref.1, bf16[128,128]{1,0:T(8,128)(2,1)} %pad.8.samp_ref, bf16[256,1024]{1,0:T(8,128)(2,1)} %w1_ref.1, bf16[1024,256]{1,0:T(8,128)(2,1)} %w2_ref.1, bf16[2,80,2048]{2,1,0:T(8,128)(2,1)} %bitcast.30, ...), custom_call_target="tpu_custom_call" | custom-call | tf_op jit(solution)/shard_map/fused_step/pallas_call | solution.py:775
  238.3 0.1 subtract_bitcast_fusion
  238.4 0.1 copy.45
  238.5 0.1 reduce-window.8
  238.7 0.1 reduce
  238.8 0.1 select_reduce_fusion
  239.0 0.1 copy.46
  239.1 0.1 copy.49
  239.2 1.0 multiply_add_fusion
  240.2 0.7 copy.50
  240.9 0.7 copy.51
  (14 shorter events, 0.1 us)
Async XLA Ops:
  0.6 8.7 %copy-start = (bf16[80,2,2048]{2,1,0:T(2,128)(2,1)S(1)}, bf16[80,2,2048]{2,1,0:T(2,128)(2,1)}, u32[]{:S(2)}) copy-start(bf16[80,2,2048]{2,1,0:T(2,128)(2,1)} %param.19) | copy-start | bytes 1966084
  0.6 9.8 %copy-start.1 = (f32[128,28]{0,1:T(8,128)S(1)}, f32[128,28]{0,1:T(8,128)}, u32[]{:S(2)}) copy-start(f32[128,28]{0,1:T(8,128)} %param.13) | copy-start | bytes 43012
  0.7 10.5 %copy-start.3 = (f32[2048]{0:T(1024)S(1)}, f32[2048]{0:T(1024)}, u32[]{:S(2)}) copy-start(f32[2048]{0:T(1024)} %param.24) | copy-start | bytes 24580
  9.4 229.4 %copy-start.4 = (s32[128]{0:T(128)S(1)}, s32[128]{0:T(128)}, u32[]{:S(2)}) copy-start(s32[128]{0:T(128)} %param.14) | copy-start | bytes 1540
  9.4 229.7 %copy-start.2 = (f32[128,28]{0,1:T(8,128)S(1)}, f32[128,28]{0,1:T(8,128)}, u32[]{:S(2)}) copy-start(f32[128,28]{0,1:T(8,128)} %param.15) | copy-start | bytes 43012

commit v2 on v1

--- a/solution.py
+++ b/solution.py
@@ -2,6 +2,7 @@
 
 import jax
 import jax.numpy as jnp
+import numpy as np
 from jax import lax
 from jax.experimental import pallas as pl
 from jax.experimental.pallas import tpu as pltpu
@@ -48,6 +49,10 @@
     alpha_bar = plan()
     now = lookup(alpha_bar, steps)[:, None]
     before = jnp.where(steps > 0, lookup(alpha_bar, jnp.maximum(steps - 1, 0)), 1.0)[:, None]
+    return denoise(sample, eps, noise, now, before)
+
+
+def denoise(sample, eps, noise, now, before):
     beta_prod = 1.0 - now
     cur_alpha = now / before
     cur_beta = 1.0 - cur_alpha
@@ -316,24 +321,31 @@
 
 
 def fused_kernel(
-    sinus_ref,
+    steps_ref,
     obs_ref,
     samp_ref,
     w1_ref,
     w2_ref,
     film_ref,
-    toep_ref,
+    conv_ref,
     gain_one_ref,
     mid_ref,
-    res_ref,
+    skip_ref,
     outw_ref,
     gain_two_ref,
-    eps_ref,
+    sel_ref,
+    noise_ref,
+    table_ref,
+    out_ref,
+    square,
     w_buf,
     a_buf,
     film_buf,
+    stage_buf,
     cond_buf,
+    conv_buf,
     toep_buf,
+    res_buf,
     gain_buf,
     own_part,
     z_recv,
@@ -349,9 +361,12 @@
     y_recv,
     fwd_send,
     fwd_recv,
+    stage_send,
+    stage_recv,
     film_send,
     film_recv,
-    filmy_sem,
+    filmy_send,
+    filmy_recv,
     filmx_send,
     filmx_recv,
     filmc_send,
@@ -360,6 +375,8 @@
     toep_recv,
     cond_send,
     cond_recv,
+    pair_send,
+    pair_recv,
     condx_send,
     condx_recv,
     zs_sem,
@@ -373,7 +390,7 @@
     f32, b16 = jnp.float32, jnp.bfloat16
     chunks = w_buf.shape[0]
     cl = w_buf.shape[2] // TAPS
-    rows = eps_ref.shape[0]
+    rows = obs_ref.shape[0]
     gw = C // GROUPS
     width = mid_ref.shape[1]
     kw = film_buf.shape[5]
@@ -402,76 +419,125 @@
             mid_ref.at[:, cols(j)], w_buf.at[j, 1], core_send.at[j], core_recv.at[j], to_c
         )
 
-    def y_copy(j):
-        return remote(mid_ref.at[:, cols(j)], w_buf.at[j, 2], y_send.at[j], y_recv.at[j], to_y)
+    def y_half(j, i):
+        some = pl.ds(i * (w_buf.shape[2] // 2), w_buf.shape[2] // 2)
+        return remote(
+            mid_ref.at[some, cols(j)],
+            w_buf.at[j, 2, some],
+            y_send.at[j, i],
+            y_recv.at[j, i],
+            to_y,
+        )
 
     def fwd_copy(j):
         return remote(w_buf.at[j, 2], w_buf.at[j, 3], fwd_send.at[j], fwd_recv.at[j], to_c)
 
-    def film_out(q, t):
-        return remote(
-            film_ref.at[t, :, pl.ds(q * kw, kw)],
-            film_buf.at[t, zi, yi, ci],
-            film_send.at[q, t],
+    near = [zi, zi + 1 - 2 * lax.rem(zi, 2), lax.rem(zi + 2, zn), zn - 1 - zi]
+    home = zi // 2
+
+    def half_cols(q):
+        return pl.ds(pl.multiple_of(q * kw, kw), kw)
+
+    def stage_copy(q):
+        return remote(
+            film_ref.at[ox, :, half_cols(q)],
+            stage_buf.at[q],
+            stage_send.at[q],
+            stage_recv.at[q],
+            to_x,
+        )
+
+    def plane_copy():
+        return remote(
+            film_ref.at[ox, :, half_cols(lax.rem(zi, 2))],
+            film_buf.at[ox, zi, yi, ci],
+            stage_send.at[lax.rem(zi, 2)],
             film_recv.at[zi],
-            {"z": 2 * xi + q, "tensor": t},
+            to_x,
+        )
+
+    def film_own(q):
+        return remote(
+            film_ref.at[xi, :, half_cols(q)],
+            film_buf.at[xi, zi, yi, ci],
+            film_send.at[0, q],
+            film_recv.at[zi],
+            {"z": 2 * xi + q},
+        )
+
+    def film_staged(q):
+        return remote(
+            stage_buf.at[q],
+            film_buf.at[xi, zi, yi, ci],
+            film_send.at[1, q],
+            film_recv.at[zi],
+            {"z": 2 * ox + q},
         )
 
     pl.semaphore_wait(barrier, len(peers))
-    y_copy(0).start()
     for q in range(2):
-        for t in range(2):
-            mine = (2 * xi + q == zi) & (xi == t)
-
-            @pl.when(mine)
-            def _():
-                pltpu.make_async_copy(
-                    film_ref.at[t, :, pl.ds(q * kw, kw)],
-                    film_buf.at[t, zi, yi, ci],
-                    film_recv.at[zi],
-                ).start()
-
-            @pl.when(jnp.logical_not(mine))
-            def _():
-                film_out(q, t).start()
-
-    home = zi // 2
-    at = pl.ds(pl.multiple_of(lax.rem(zi, 2) * kw, kw), kw)
-
-    def toep_copy():
-        return remote(
-            toep_ref.at[:, :, at], toep_buf, toep_send.at[0], toep_recv.at[0], to_x
-        )
+        mine = 2 * xi + q == zi
+
+        @pl.when(mine)
+        def _():
+            plane_copy().start()
+            pltpu.make_async_copy(
+                film_ref.at[xi, :, half_cols(q)], film_buf.at[xi, zi, yi, ci], film_recv.at[zi]
+            ).start()
+
+        @pl.when(jnp.logical_not(mine))
+        def _():
+            stage_copy(q).start()
+            film_own(q).start()
+
+    y_half(0, 0).start()
+
+    at = half_cols(lax.rem(zi, 2))
+
+    def conv_copy():
+        return remote(conv_ref.at[:, :, at], conv_buf, toep_send.at[0], toep_recv.at[0], to_x)
 
     def gain_copy():
         return remote(gain_one_ref.at[:, at], gain_buf, toep_send.at[1], toep_recv.at[1], to_x)
 
     @pl.when(xi == home)
     def _():
-        toep_copy().start()
+        conv_copy().start()
         gain_copy().start()
-        pltpu.make_async_copy(toep_ref.at[:, :, at], toep_buf, toep_recv.at[0]).start()
+        pltpu.make_async_copy(conv_ref.at[:, :, at], conv_buf, toep_recv.at[0]).start()
         pltpu.make_async_copy(gain_one_ref.at[:, at], gain_buf, toep_recv.at[1]).start()
 
-    hidden = mish(jnp.dot(sinus_ref[...], w1_ref[...], preferred_element_type=f32)).astype(b16)
+    half = rows // 2
+    sw = w2_ref.shape[1]
+    cond_obs = mish(obs_ref[...].astype(f32)).astype(b16)
+    square[...] = jnp.zeros_like(square)
+    square[: HORIZON * ACT] = samp_ref[...]
+    samp = square[...].T.astype(b16)
+    count = w1_ref.shape[0] // 2
+    index = lax.broadcasted_iota(jnp.int32, (count, rows), 0).astype(f32)
+    freqs = jnp.exp(index * (-math.log(10000.0) / (count - 1)))
+    angles = steps_ref[...].astype(f32) * freqs
+    sinus = jnp.concatenate([jnp.sin(angles), jnp.cos(angles)], axis=0).astype(b16)
+    hidden = mish(
+        lax.dot_general(
+            sinus, w1_ref[...], (((0,), (0,)), ((), ())), preferred_element_type=f32
+        )
+    ).astype(b16)
     step_feat = jnp.dot(hidden, w2_ref[...], preferred_element_type=f32)
-    half = rows // 2
-    sw = step_feat.shape[1]
     cond_step = mish(step_feat).astype(b16)
-    cond_obs = mish(obs_ref[...].astype(f32)).astype(b16)
     for i in range(2):
         part = slice(i * half, (i + 1) * half)
         cond_buf[zi, i, :, :sw] = cond_step[part]
         cond_buf[zi, i, :, sw:feat] = cond_obs[part]
-        cond_buf[zi, i, :, feat:] = samp_ref[part]
+        cond_buf[zi, i, :, feat:] = samp[part]
 
     def cond_copy(dz):
         return remote(
             cond_buf.at[zi, xi],
             cond_buf.at[zi, xi],
-            cond_send.at[dz - 1],
+            cond_send.at[dz - 2],
             cond_recv.at[zi],
-            {"z": lax.rem(zi + dz, zn)},
+            {"z": near[dz]},
         )
 
     def condx_copy(z, i):
@@ -484,69 +550,123 @@
             cond_buf.at[z, xi], cond_buf.at[z, xi], cond_send.at[0], cond_recv.at[z], to_x
         )
 
-    for dz in range(1, zn):
-        cond_copy(dz).start()
+    for q in range(2):
+
+        @pl.when(2 * ox + q != zi)
+        def _():
+            stage_copy(q).wait_recv()
+            film_staged(q).start()
+
+    def cond_pair(i):
+        return remote(
+            cond_buf.at[zi, i],
+            cond_buf.at[zi, i],
+            pair_send.at[i],
+            pair_recv.at[i],
+            {"z": near[1]},
+        )
+
+    for i in range(2):
+        cond_pair(i).start()
+    for k in range(2, zn):
+        cond_copy(k).start()
 
     @pl.loop(0, chunks)
     def _(j):
         own_copy(j).start()
         core_copy(j).start()
 
-    def film_x(i, t, y):
-        piece = film_buf.at[t, :, y, ci]
-        return remote(piece, piece, filmx_send.at[i], filmx_recv.at[i], to_x)
-
-    def film_y(y):
-        piece = film_buf.at[xi, :, y, ci]
-        return remote(piece, piece, filmy_sem.at[0], filmy_sem.at[1], to_y)
-
-    def film_c(i, t, y, c):
-        piece = film_buf.at[t, :, y, c]
-        return remote(piece, piece, filmc_send.at[i], filmc_recv.at[i], to_c)
-
-    for z in range(zn):
+    def film_in(z):
         piece = film_buf.at[xi, z, yi, ci]
-        remote(piece, piece, film_send.at[0, 0], film_recv.at[z], to_x).wait_recv()
-    film_y(yi).start()
-    film_x(0, xi, yi).start()
-    film_c(0, xi, yi, ci).start()
-
-    @pl.loop(1, chunks)
-    def _(j):
-        y_copy(j).start()
-
-    for dz in range(1, zn):
-        z = lax.rem(zi + dz, zn)
+        return remote(piece, piece, film_send.at[0, 0], film_recv.at[z], to_x)
+
+    def film_y(z, t, y):
+        piece = film_buf.at[t, z, y, ci]
+        return remote(piece, piece, filmy_send.at[z], filmy_recv.at[z], to_y)
+
+    def film_x(z, t, y):
+        piece = film_buf.at[t, z, y, ci]
+        k = (y + yi) % 2
+        return remote(piece, piece, filmx_send.at[k, z], filmx_recv.at[k, z], to_x)
+
+    def film_c(z, t, y, c):
+        piece = film_buf.at[t, z, y, c]
+        k = 2 * ((t + xi) % 2) + (y + yi) % 2
+        return remote(piece, piece, filmc_send.at[k, z], filmc_recv.at[k, z], to_c)
+
+    def arrived(z):
+        film_in(z).wait_recv()
+        film_y(z, xi, yi).start()
+        film_x(z, xi, yi).start()
+        film_c(z, xi, yi, ci).start()
+
+    def crossed(z):
+        film_y(z, xi, oy).wait_recv()
+        film_x(z, xi, oy).start()
+        film_c(z, xi, oy, ci).start()
+
+    def known(z):
         cond_in(z).wait_recv()
         condx_copy(z, xi).start()
-    film_y(oy).wait_recv()
-    film_x(1, xi, oy).start()
-    film_c(1, xi, oy, ci).start()
-    film_x(0, ox, yi).wait_recv()
-    film_c(2, ox, yi, ci).start()
-    film_x(1, ox, oy).wait_recv()
-    film_c(3, ox, oy, ci).start()
-    toep_copy().wait_recv()
+
+    arrived(near[0])
+    y_half(0, 1).start()
+    arrived(near[1])
+    crossed(near[0])
+    arrived(near[2])
+    crossed(near[1])
+    y_half(1, 0).start()
+    arrived(near[3])
+    y_half(1, 1).start()
+    crossed(near[2])
+
+    @pl.loop(2, chunks)
+    def _(j):
+        for i in range(2):
+            y_half(j, i).start()
+
+    known(near[2])
+    crossed(near[3])
+    known(near[3])
+    conv_copy().wait_recv()
     gain_copy().wait_recv()
-    for dz in range(1, zn):
-        condx_copy(lax.rem(zi + dz, zn), ox).wait_recv()
-    for i, (t, y) in enumerate(((xi, yi), (xi, oy), (ox, yi), (ox, oy))):
-        film_c(i, t, y, oc).wait_recv()
+    total = None
+    for k in range(TAPS):
+        term = jnp.dot(sel_ref[k], conv_buf[k], preferred_element_type=f32)
+        total = term if total is None else total + term
+    toep_buf[...] = total.astype(b16)
+    res_buf[...] = jnp.dot(sel_ref[mid], skip_ref[...], preferred_element_type=f32).astype(b16)
+    for z in near:
+        film_x(z, ox, yi).wait_recv()
+        film_c(z, ox, yi, ci).start()
+    for z in near:
+        film_x(z, ox, oy).wait_recv()
+        film_c(z, ox, oy, ci).start()
+    for z in near[2:]:
+        condx_copy(z, ox).wait_recv()
+    for i in range(2):
+        piece = cond_buf.at[near[1], i]
+        remote(piece, piece, pair_send.at[i], pair_recv.at[i], to_x).wait_recv()
+    for z in near:
+        for t in range(2):
+            for y in range(2):
+                film_c(z, t, y, oc).wait_recv()
 
     per = gw // cl
     inner = film_buf.shape[1] * film_buf.shape[2] * film_buf.shape[3] * film_buf.shape[4]
-
-    @pl.loop(0, zn)
-    def _(z):
+    pad = sel_ref.shape[1] // HORIZON
+
+    def first(r, ab):
+        z = ab * SPLIT + r
         cond = cond_buf[z].reshape(rows, cond_buf.shape[3])
-        x = cond[:, feat : feat + toep_buf.shape[1]]
+        x = cond[:, feat : feat + pad]
         cond = cond[:, :feat]
-        ab = z // SPLIT
-        r = lax.rem(z, SPLIT)
         for g in range(kw // gw):
             span = slice(g * gw, (g + 1) * gw)
             hs = [
-                jnp.dot(x, toep_buf[h, :, span], preferred_element_type=f32)
+                jnp.dot(
+                    x, toep_buf[h * pad : (h + 1) * pad, span], preferred_element_type=f32
+                )
                 for h in range(HORIZON)
             ]
             hs = normed(hs, gain_buf[0:1, span])
@@ -571,58 +691,63 @@
     order = [yi * 2 + ci, yi * 2 + oc, oy * 2 + ci, oy * 2 + oc]
     steps = chunks * SPLIT
     ring = own_part.shape[0]
+    zring = z_send.shape[1]
     ends = (zi == 0) | (zi == zn - 1)
 
-    def z_copy(d, s):
-        k = lax.rem(s, ring)
-        return remote(
-            z_send.at[d, k],
-            z_recv.at[d, s],
-            zs_sem.at[d, k],
-            zr_sem.at[d, s],
+    def z_copy(d, s, h):
+        k = lax.rem(s, zring)
+        return remote(
+            z_send.at[d, k, h],
+            z_recv.at[d, s, h],
+            zs_sem.at[d, k, h],
+            zr_sem.at[d, s, h],
             {"z": jnp.maximum(zi - 1, 0) if d == 0 else jnp.minimum(zi + 1, zn - 1)},
         )
 
     def flow(d, now):
-        lag = zn - 1 - zi if d == 0 else zi
-        s = now - lag
+        pos = zn - 1 - zi if d == 0 else zi
+        s = now - pos - pos // (zn - 1)
         k = lax.rem(s + ring, ring)
+        kz = lax.rem(s + zring, zring)
 
         @pl.when((s >= 0) & (s < steps))
         def _():
-            @pl.when(lag > 0)
-            def _():
-                z_copy(d, s).wait_recv()
-
-            @pl.when(lag == zn - 1)
+            @pl.when(pos == zn - 1)
             def _():
                 for h in range(HORIZON):
+                    z_copy(d, s, h).wait_recv()
                     last[lax.rem(s, SPLIT), lax.rem(s // SPLIT, 2), h] = own_part[
                         k, d, h
                     ] + z_recv[d, s, h].astype(f32)
 
-            @pl.when(lag < zn - 1)
+            @pl.when((pos < zn - 1) & (s >= zring))
             def _():
-                @pl.when(s >= ring)
-                def _():
-                    z_copy(d, s - ring).wait_send()
-
-                @pl.when(lag == 0)
-                def _():
-                    for h in range(HORIZON):
-                        z_send[d, k, h] = own_part[k, d, h].astype(b16)
-
-                @pl.when(lag > 0)
-                def _():
-                    for h in range(HORIZON):
-                        z_send[d, k, h] = (
-                            own_part[k, d, h] + z_recv[d, s, h].astype(f32)
-                        ).astype(b16)
-
-                z_copy(d, s).start()
-
-    @pl.loop(0, steps + zn - 1)
+                for h in range(HORIZON):
+                    z_copy(d, s - zring, h).wait_send()
+
+            @pl.when(pos == 0)
+            def _():
+                for h in range(HORIZON):
+                    z_send[d, kz, h] = own_part[k, d, h].astype(b16)
+                    z_copy(d, s, h).start()
+
+            @pl.when((pos > 0) & (pos < zn - 1))
+            def _():
+                for h in range(HORIZON):
+                    z_copy(d, s, h).wait_recv()
+                    z_send[d, kz, h] = (
+                        own_part[k, d, h] + z_recv[d, s, h].astype(f32)
+                    ).astype(b16)
+                    z_copy(d, s, h).start()
+
+    @pl.loop(0, steps + zn)
     def _(now):
+        @pl.when(now < SPLIT)
+        def _():
+            @pl.loop(0, 2)
+            def _(ab):
+                first(now, ab)
+
         @pl.when(now < steps)
         def _():
             j = now // SPLIT
@@ -631,7 +756,8 @@
 
             @pl.when(r == 0)
             def _():
-                y_copy(j).wait_recv()
+                for i in range(2):
+                    y_half(j, i).wait_recv()
                 fwd_copy(j).start()
                 own_copy(j).wait()
                 core_copy(j).wait_recv()
@@ -656,7 +782,7 @@
 
         flow(1, now)
         flow(0, now)
-        done = now - (zn - 1)
+        done = now - zn
 
         @pl.when((done >= 0) & ends & (lax.rem(done // SPLIT, 2) == 1))
         def _():
@@ -668,11 +794,18 @@
                 jnp.concatenate([last[r, 0, h], last[r, 1, h]], axis=1) for h in range(HORIZON)
             ]
             hs = normed(hs, gain_two_ref[0:1, span])
-            x = cond_buf[z, :, :, feat:].reshape(rows, LANES)[:, : res_ref.shape[1]]
+            x = cond_buf[z, :, :, feat:].reshape(rows, LANES)[:, :pad]
             for h in range(HORIZON):
-                skip = jnp.dot(x, res_ref[h, :, span], preferred_element_type=f32)
+                skip = jnp.dot(
+                    x, res_buf[h * pad : (h + 1) * pad, span], preferred_element_type=f32
+                )
                 act = (mish(hs[h]) + skip).astype(b16)
-                eps_acc[r, h] += jnp.dot(act, outw_ref[span, :], preferred_element_type=f32)
+                eps_acc[r, h] += lax.dot_general(
+                    act,
+                    outw_ref[:, span],
+                    (((1,), (1,)), ((), ())),
+                    preferred_element_type=f32,
+                )
 
     end = (zi // SPLIT) * (zn - 1)
 
@@ -690,9 +823,12 @@
 
         @pl.when(ends)
         def _():
-            total = eps_acc[r, 0]
-            for h in range(1, HORIZON):
-                total = total + pltpu.roll(eps_acc[r, h], h * ACT, 1)
+            total = jnp.concatenate(
+                [eps_acc[r, h] for h in range(HORIZON)]
+                + [jnp.zeros((rows, LANES - HORIZON * ACT), f32)],
+                axis=1,
+            )
+            total = total.T[: eps_send.shape[1]]
             eps_send[r] = total
 
             @pl.when(z == zi)
@@ -713,7 +849,15 @@
                 eps_send.at[0], eps_recv.at[t], eps_ssem.at[0, 0], eps_rsem.at[t], to_x
             ).wait_recv()
 
-    eps_ref[...] = eps_recv[0] + eps_recv[1]
+    eps = (eps_recv[0] + eps_recv[1])[: HORIZON * ACT]
+    out_ref[0, : HORIZON * ACT] = eps
+    when = steps_ref[...]
+    spots = lax.broadcasted_iota(jnp.int32, square.shape, 0)
+    table = jnp.broadcast_to(table_ref[...], square.shape).T
+    now = jnp.sum(jnp.where(spots == when, table, 0.0), axis=0, keepdims=True)
+    before = jnp.sum(jnp.where(spots == when - 1, table, 0.0), axis=0, keepdims=True)
+    before = jnp.where(when > 0, before, 1.0)
+    out_ref[1, : HORIZON * ACT] = denoise(samp_ref[...], eps, noise_ref[...], now, before)
 
     for r in range(SPLIT):
         z = (zi // (zn - 1)) * SPLIT + r
@@ -727,38 +871,53 @@
 
         @pl.when((zi < zn - 1) if d else (zi > 0))
         def _():
-            for s in range(steps - ring, steps):
-                z_copy(d, s).wait_send()
+            for s in range(steps - zring, steps):
+                for h in range(HORIZON):
+                    z_copy(d, s, h).wait_send()
 
     @pl.loop(0, chunks)
     def _(j):
-        y_copy(j).wait_send()
+        for i in range(2):
+            y_half(j, i).wait_send()
         core_copy(j).wait_send()
         fwd_copy(j).wait_send()
 
     for q in range(2):
-        for t in range(2):
-
-            @pl.when((2 * xi + q != zi) | (xi != t))
-            def _():
-                film_out(q, t).wait_send()
+        mine = 2 * xi + q == zi
+
+        @pl.when(mine)
+        def _():
+            plane_copy().wait_send()
+
+        @pl.when(jnp.logical_not(mine))
+        def _():
+            stage_copy(q).wait_send()
+            film_own(q).wait_send()
+
+        @pl.when(2 * ox + q != zi)
+        def _():
+            film_staged(q).wait_send()
 
     @pl.when(xi == home)
     def _():
-        toep_copy().wait_send()
+        conv_copy().wait_send()
         gain_copy().wait_send()
 
-    for dz in range(1, zn):
-        cond_copy(dz).wait_send()
-        condx_copy(lax.rem(zi + dz, zn), xi).wait_send()
-    film_y(yi).wait_send()
-    film_x(0, xi, yi).wait_send()
-    film_x(1, xi, oy).wait_send()
-    for i, (t, y) in enumerate(((xi, yi), (xi, oy), (ox, yi), (ox, oy))):
-        film_c(i, t, y, ci).wait_send()
-
-
-def fused(sinus, obs, samp, w1, w2, film, toep, gain_one, weights, res, outw, gain_two):
+    for i in range(2):
+        cond_pair(i).wait_send()
+    for k in range(2, zn):
+        cond_copy(k).wait_send()
+        condx_copy(near[k], xi).wait_send()
+    for z in near:
+        film_y(z, xi, yi).wait_send()
+        film_x(z, xi, yi).wait_send()
+        film_x(z, xi, oy).wait_send()
+        for y in range(2):
+            for t in range(2):
+                film_c(z, t, y, ci).wait_send()
+
+
+def fused(steps, obs, samp, w1, w2, film, conv, gain_one, weights, skip, outw, gain_two, sel, noise, table):
     rows = obs.shape[0]
     depth, width = weights.shape
     chunks = width // CHUNK
@@ -766,53 +925,63 @@
     kw = cl * 4
     fr = film.shape[1]
     feat = w2.shape[1] + obs.shape[1]
-    steps = chunks * SPLIT
-    ring = DEPTH_PARTS
+    count = chunks * SPLIT
+    ring = DEPTH_PARTS + 1
+    zring = 4
     b16, f32 = jnp.bfloat16, jnp.float32
     dma = pltpu.SemaphoreType.DMA
     vm = pl.BlockSpec(memory_space=pltpu.VMEM)
     hbm = pl.BlockSpec(memory_space=pl.ANY)
     return pl.pallas_call(
         fused_kernel,
-        out_shape=jax.ShapeDtypeStruct((rows, LANES), f32),
-        in_specs=[vm, vm, vm, vm, vm, hbm, hbm, hbm, hbm, vm, vm, vm],
+        out_shape=jax.ShapeDtypeStruct((2, 32, rows), f32),
+        in_specs=[vm, vm, vm, vm, vm, hbm, hbm, hbm, hbm, vm, vm, vm, vm, vm, vm],
         out_specs=vm,
         scratch_shapes=[
+            pltpu.VMEM((LANES, LANES), f32),
             pltpu.VMEM((chunks, 4, depth, CHUNK), b16),
             pltpu.VMEM((4, SPLIT, 2, rows, HORIZON * cl), b16),
             pltpu.VMEM((2, DEPTH_PARTS, 2, 2, fr, kw), b16),
+            pltpu.VMEM((2, fr, kw), b16),
             pltpu.VMEM((DEPTH_PARTS, 2, rows // 2, feat + LANES), b16),
-            pltpu.VMEM((HORIZON, toep.shape[1], kw), b16),
+            pltpu.VMEM((TAPS, ACT, kw), b16),
+            pltpu.VMEM((sel.shape[1], kw), b16),
+            pltpu.VMEM((sel.shape[1], width), b16),
             pltpu.VMEM((gain_one.shape[0], kw), f32),
             pltpu.VMEM((ring, 2, HORIZON, rows, CHUNK), f32),
-            pltpu.VMEM((2, steps, HORIZON, rows, CHUNK), b16),
-            pltpu.VMEM((2, ring, HORIZON, rows, CHUNK), b16),
+            pltpu.VMEM((2, count, HORIZON, rows, CHUNK), b16),
+            pltpu.VMEM((2, zring, HORIZON, rows, CHUNK), b16),
             pltpu.VMEM((SPLIT, 2, HORIZON, rows, CHUNK), f32),
-            pltpu.VMEM((SPLIT, HORIZON, rows, LANES), f32),
-            pltpu.VMEM((SPLIT, rows, LANES), f32),
-            pltpu.VMEM((2, rows, LANES), f32),
+            pltpu.VMEM((SPLIT, HORIZON, rows, ACT), f32),
+            pltpu.VMEM((SPLIT, 32, rows), f32),
+            pltpu.VMEM((2, 32, rows), f32),
             dma((chunks,)),
             dma((chunks,)),
             dma((chunks,)),
+            dma((chunks, 2)),
+            dma((chunks, 2)),
             dma((chunks,)),
             dma((chunks,)),
-            dma((chunks,)),
-            dma((chunks,)),
+            dma((2,)),
+            dma((2,)),
             dma((2, 2)),
+            dma((DEPTH_PARTS,)),
+            dma((DEPTH_PARTS,)),
+            dma((DEPTH_PARTS,)),
+            dma((2, DEPTH_PARTS)),
+            dma((2, DEPTH_PARTS)),
+            dma((4, DEPTH_PARTS)),
+            dma((4, DEPTH_PARTS)),
+            dma((2,)),
+            dma((2,)),
+            dma((DEPTH_PARTS - 2,)),
             dma((DEPTH_PARTS,)),
             dma((2,)),
             dma((2,)),
-            dma((2,)),
-            dma((4,)),
-            dma((4,)),
-            dma((2,)),
-            dma((2,)),
-            dma((DEPTH_PARTS - 1,)),
             dma((DEPTH_PARTS,)),
             dma((DEPTH_PARTS,)),
-            dma((DEPTH_PARTS,)),
-            dma((2, ring)),
-            dma((2, steps)),
+            dma((2, zring, HORIZON)),
+            dma((2, count, HORIZON)),
             dma((SPLIT, 2)),
             dma((2,)),
         ],
@@ -820,16 +989,19 @@
             collective_id=0, has_side_effects=True, vmem_limit_bytes=VMEM
         ),
         name="fused_step",
-    )(sinus, obs, samp, w1, w2, film, toep, gain_one, weights, res, outw, gain_two)
-
-
-def spread(blocks, lead):
-    width = next(b for b in blocks if b is not None).shape[1]
-    rows = []
-    for p in range(HORIZON):
-        rows.append(blocks[p] if blocks[p] is not None else jnp.zeros((ACT, width), lead))
-    rows.append(jnp.zeros((32 - HORIZON * ACT, width), lead))
-    return jnp.concatenate(rows, axis=0)
+    )(steps, obs, samp, w1, w2, film, conv, gain_one, weights, skip, outw, gain_two, sel, noise, table)
+
+
+def selection(dtype):
+    pad = 32
+    table = np.zeros((TAPS, HORIZON * pad, ACT), np.float32)
+    for h in range(HORIZON):
+        for p in range(HORIZON):
+            k = p - h + TAPS // 2
+            for a in range(ACT):
+                if 0 <= k < TAPS:
+                    table[k, h * pad + p * ACT + a, a] = 1.0
+    return jnp.asarray(table, dtype)
 
 
 def fused_body(
@@ -848,45 +1020,25 @@
     gain_two,
 ):
     width = conv_in_w.shape[2]
-    lead = conv_in_w.dtype
-    taps = lambda h, p: p - h + TAPS // 2
-    toep = jnp.stack(
-        [
-            spread(
-                [
-                    conv_in_w[taps(h, p)] if 0 <= taps(h, p) < TAPS else None
-                    for p in range(HORIZON)
-                ],
-                lead,
-            )
-            for h in range(HORIZON)
-        ]
-    )
-    blank = jnp.zeros((ACT, width), lead)
-    res = jnp.stack(
-        [
-            spread([residual_w if p == h else blank for p in range(HORIZON)], lead)
-            for h in range(HORIZON)
-        ]
-    )
-    samp = jnp.pad(
-        noisy_sample.astype(lead), ((0, 0), (0, LANES - noisy_sample.shape[1]))
-    )
-    eps = fused(
-        sinusoid(timestep).astype(lead),
+    table = plan()
+    both = fused(
+        timestep[None, :],
         obs_feat,
-        samp,
+        noisy_sample.T,
         step_w1,
         step_w2,
         jnp.transpose(film_weight, (1, 0, 2)),
-        toep,
-        jnp.broadcast_to(gain_one[None, :], (8, width)),
+        conv_in_w,
+        gain_one[None, :],
         conv_mid_w.reshape(-1, width),
-        res,
-        jnp.pad(out_w, ((0, 0), (0, LANES - ACT))),
+        residual_w,
+        out_w.T,
         gain_two[None, :],
-    )[:, : HORIZON * ACT]
-    return (eps, denoise_step(noisy_sample, eps, noise, timestep))
+        selection(conv_in_w.dtype),
+        noise.T,
+        jnp.pad(table, (0, LANES - table.shape[0]))[None, :],
+    )
+    return (both[0, : HORIZON * ACT].T, both[1, : HORIZON * ACT].T)
 
 
 def solution(mesh):

time: 242 us -> 187 us (0.77)
  Pallas kernels: 226 us -> 182 us
  other arithmetic: 5.39 us -> 0.38 us
  local copies, waits for them, and re-layouts: 8.92 us -> 4.12 us
    pallas_call x1, Pallas kernels: 226 us -> 182 us  [fused(): pl.pallas_call(fused_kernel, out_shape=jax.ShapeDtypeStruct((2, 32, rows)...]
    another operation x6 -> x3, other arithmetic: 2.84 us -> 0.33 us  [the longest x1 1.13 us: fused_body(): jnp.stack([spread([conv_in_w[taps(h, p)] if 0 <= taps(h, p) < TAPS else N...]
where the time goes in v2:
time: 187 us
  Pallas kernels  182 us (97%)
  local copies, waits for them, and re-layouts  4.12 us (2%)
    pallas_call x1, Pallas kernels, fused(): pl.pallas_call(fused_kernel, out_shape=jax.ShapeDtypeStruct((2, 32, rows)...  182 us

profile of v2, /device:TPU:0, one launch (start us, length us, event | category | flops | bytes accessed | tf_op | source)
XLA Modules:
  0.0 186.8 jit_solution(5489627167455225692)
XLA Ops:
  0.7 0.1 subtract_bitcast_fusion
  0.8 0.1 copy.19
  0.9 0.1 reduce-window.9
  1.0 0.1 reduce
  1.1 0.5 pad_bitcast_fusion.table_ref
  1.7 2.1 %copy.21 = bf16[80,2,2048]{2,0,1:T(8,128)(2,1)} copy(bf16[80,2,2048]{2,1,0:T(2,128)(2,1)} %param.20) | data formatting | bytes 1310720 | tf_op args[6]
  3.8 181.6 %fused_step.1 = f32[2,32,128]{2,1,0:T(8,128)} custom-call(s32[1,128]{1,0:T(1,128)} %bitcast.29, bf16[128,1024]{1,0:T(8,128)(2,1)} %obs_ref.1, f32[28,128]{1,0:T(8,128)} %bitcast.25, bf16[256,1024]{1,0:T(8,128)(2,1)} %w1_ref.1, bf16[1024,256]{1,0:T(8,128)(2,1)} %w2_ref.1, bf16[2,80,2048]{2,1,0:T(8,128)(2,1)} %bitcast.23, bf16[5,7,2048]{2,1,0:T(8,128)(2,1)} %conv_ref.1, ...), custom_call_target="tpu_custom_call" | custom-call | tf_op jit(solution)/shard_map/fused_step/pallas_call | solution.py:935
  185.4 1.3 slice_bitcast_fusion
  (1 shorter events, 0.0 us)

commit v3 on v2

--- a/solution.py
+++ b/solution.py
@@ -492,6 +492,11 @@
 
     y_half(0, 0).start()
 
+    @pl.loop(0, chunks)
+    def _(j):
+        own_copy(j).start()
+        core_copy(j).start()
+
     at = half_cols(lax.rem(zi, 2))
 
     def conv_copy():
@@ -550,6 +555,42 @@
             cond_buf.at[z, xi], cond_buf.at[z, xi], cond_send.at[0], cond_recv.at[z], to_x
         )
 
+    def film_in(z):
+        piece = film_buf.at[xi, z, yi, ci]
+        return remote(piece, piece, film_send.at[0, 0], film_recv.at[z], to_x)
+
+    def film_y(z, t, y):
+        piece = film_buf.at[t, z, y, ci]
+        return remote(piece, piece, filmy_send.at[z], filmy_recv.at[z], to_y)
+
+    def film_x(z, t, y):
+        piece = film_buf.at[t, z, y, ci]
+        k = (y + yi) % 2
+        return remote(piece, piece, filmx_send.at[k, z], filmx_recv.at[k, z], to_x)
+
+    def film_c(z, t, y, c):
+        piece = film_buf.at[t, z, y, c]
+        k = 2 * ((t + xi) % 2) + (y + yi) % 2
+        return remote(piece, piece, filmc_send.at[k, z], filmc_recv.at[k, z], to_c)
+
+    def arrived(z):
+        film_in(z).wait_recv()
+        film_y(z, xi, yi).start()
+        film_x(z, xi, yi).start()
+        film_c(z, xi, yi, ci).start()
+
+    def crossed(z):
+        film_y(z, xi, oy).wait_recv()
+        film_x(z, xi, oy).start()
+        film_c(z, xi, oy, ci).start()
+
+    def known(z):
+        cond_in(z).wait_recv()
+        condx_copy(z, xi).start()
+
+    arrived(near[0])
+    y_half(0, 1).start()
+
     for q in range(2):
 
         @pl.when(2 * ox + q != zi)
@@ -571,46 +612,6 @@
     for k in range(2, zn):
         cond_copy(k).start()
 
-    @pl.loop(0, chunks)
-    def _(j):
-        own_copy(j).start()
-        core_copy(j).start()
-
-    def film_in(z):
-        piece = film_buf.at[xi, z, yi, ci]
-        return remote(piece, piece, film_send.at[0, 0], film_recv.at[z], to_x)
-
-    def film_y(z, t, y):
-        piece = film_buf.at[t, z, y, ci]
-        return remote(piece, piece, filmy_send.at[z], filmy_recv.at[z], to_y)
-
-    def film_x(z, t, y):
-        piece = film_buf.at[t, z, y, ci]
-        k = (y + yi) % 2
-        return remote(piece, piece, filmx_send.at[k, z], filmx_recv.at[k, z], to_x)
-
-    def film_c(z, t, y, c):
-        piece = film_buf.at[t, z, y, c]
-        k = 2 * ((t + xi) % 2) + (y + yi) % 2
-        return remote(piece, piece, filmc_send.at[k, z], filmc_recv.at[k, z], to_c)
-
-    def arrived(z):
-        film_in(z).wait_recv()
-        film_y(z, xi, yi).start()
-        film_x(z, xi, yi).start()
-        film_c(z, xi, yi, ci).start()
-
-    def crossed(z):
-        film_y(z, xi, oy).wait_recv()
-        film_x(z, xi, oy).start()
-        film_c(z, xi, oy, ci).start()
-
-    def known(z):
-        cond_in(z).wait_recv()
-        condx_copy(z, xi).start()
-
-    arrived(near[0])
-    y_half(0, 1).start()
     arrived(near[1])
     crossed(near[0])
     arrived(near[2])
@@ -780,8 +781,16 @@
                 for d in range(2):
                     own_part[k, d, h] = acc[d * rows : (d + 1) * rows]
 
-        flow(1, now)
+        @pl.when(zi < zn // 2)
+        def _():
+            flow(1, now)
+
         flow(0, now)
+
+        @pl.when(zi >= zn // 2)
+        def _():
+            flow(1, now)
+
         done = now - zn
 
         @pl.when((done >= 0) & ends & (lax.rem(done // SPLIT, 2) == 1))

time: 187 us -> 183 us (0.979)
  Pallas kernels: 182 us -> 178 us
    pallas_call x1, Pallas kernels: 182 us -> 178 us  [fused(): pl.pallas_call(fused_kernel, out_shape=jax.ShapeDtypeStruct((2, 32, rows)...]
where the time goes in v3:
time: 183 us
  Pallas kernels  178 us (97%)
  local copies, waits for them, and re-layouts  4.12 us (2%)
    pallas_call x1, Pallas kernels, fused(): pl.pallas_call(fused_kernel, out_shape=jax.ShapeDtypeStruct((2, 32, rows)...  178 us

profile of v3, /device:TPU:0, one launch (start us, length us, event | category | flops | bytes accessed | tf_op | source)
XLA Modules:
  0.0 182.9 jit_solution(12343526198847325925)
XLA Ops:
  0.7 0.1 subtract_bitcast_fusion
  0.8 0.1 copy.19
  0.9 0.1 reduce-window.9
  1.0 0.1 reduce
  1.1 0.5 pad_bitcast_fusion.table_ref
  1.7 2.1 %copy.21 = bf16[80,2,2048]{2,0,1:T(8,128)(2,1)} copy(bf16[80,2,2048]{2,1,0:T(2,128)(2,1)} %param.20) | data formatting | bytes 1310720 | tf_op args[6]
  3.8 177.8 %fused_step.1 = f32[2,32,128]{2,1,0:T(8,128)} custom-call(s32[1,128]{1,0:T(1,128)} %bitcast.29, bf16[128,1024]{1,0:T(8,128)(2,1)} %obs_ref.1, f32[28,128]{1,0:T(8,128)} %bitcast.25, bf16[256,1024]{1,0:T(8,128)(2,1)} %w1_ref.1, bf16[1024,256]{1,0:T(8,128)(2,1)} %w2_ref.1, bf16[2,80,2048]{2,1,0:T(8,128)(2,1)} %bitcast.23, bf16[5,7,2048]{2,1,0:T(8,128)(2,1)} %conv_ref.1, ...), custom_call_target="tpu_custom_call" | custom-call | tf_op jit(solution)/shard_map/fused_step/pallas_call | solution.py:944
  181.5 1.3 slice_bitcast_fusion
  (1 shorter events, 0.0 us)
